TPU v7x, 32 devices: a whole 2x2x4 slice. The times are simulated.
32 devices in a mesh: row: 4 (over x, core), col: 4 (over z), depth: 2 (over y).
Axes of the slice: x: 2, y: 2, z: 4, core: 2. Of those that a mesh axis runs over, the one named last changes fastest.
Arguments:
- acts: bfloat16 [256, 32768], P('depth', 'row'), may hold values from -6 to 6
- act_mask: int32 [256, 256], P('depth', 'row'), may hold values 0 or 1
- w1: bfloat16 [256, 32, 128, 128], P(('row', 'depth'), 'col'), may hold values from -0.09375 to 0.09375
- cols1: int32 [256, 32], P('row', 'col'), may hold values from 0 to 255, as said below
- bias1: float32 [32768], P('col'), may hold values from -3 to 3
- mask2: int32 [256, 256], P('depth', 'col'), may hold values 0 or 1
- w2: bfloat16 [256, 32, 128, 128], P(('col', 'depth'), 'row'), may hold values from -0.1875 to 0.1875
- cols2: int32 [256, 32], P('col', 'row'), may hold values from 0 to 255, as said below
- bias2: float32 [32768], P(('row', 'col')), may hold values from -3 to 3
Outputs:
- result: bfloat16 [256, 32768], P('depth', ('row', 'col'))
Inputs may be any that keep to these rules, and one draw needn't show every extreme that they name: `cols1`: in each of the 256 block rows the 32 entries name different block columns, and for every g the entries g * 8 to g * 8 + 7 lie among block columns g * 64 to g * 64 + 63. `cols2`: in each of the 256 block rows the 32 entries name different block columns, and for every g the entries g * 8 to g * 8 + 7 lie among block columns g * 64 to g * 64 + 63.
All inputs are finite; a program needn't handle non-finite values. No bound on the sum of `act_mask` or of `mask2` on one device may be relied on, other than what follows from the above.
Results may differ from a plain program's by a relative error of at most 0.0047.
Values may be sent and summed in bfloat16 or wider, within the bound.
A program may use at most 128 MiB of HBM per device.

v0:
```python
import jax
import jax.numpy as jnp
from jax import lax
from jax.sharding import PartitionSpec as P


def fold_function(inputs, targets, stride):

    def add_tiles(running_total, tiles, first_row):

        def advance(number, total):
            offset = number * stride
            block_list = lax.dynamic_slice_in_dim(tiles, offset, stride, 0)
            incoming_rows = lax.dynamic_slice_in_dim(inputs, offset, stride, 1)
            wanted = lax.dynamic_slice_in_dim(targets, offset, stride, 0)
            product = jnp.einsum(
                "tws,wish->twih", incoming_rows, block_list, preferred_element_type=jnp.float32
            )
            flat_product = product.reshape(product.shape[0], -1, product.shape[-1])
            return total.at[:, wanted.reshape(-1)].add(flat_product)

        return lax.fori_loop(0, tiles.shape[0] // stride, advance, running_total)

    return add_tiles


def on_device(acts, act_mask, w1, cols1, bias1, mask2, w2, cols2, bias2):
    block = w1.shape[-1]
    rows_dev = acts.shape[0]
    row_blocks = act_mask.shape[1]
    col_blocks = mask2.shape[1]
    row_index = lax.axis_index("row")
    col_index = lax.axis_index("col")
    masked = acts.reshape(rows_dev, row_blocks, block) * act_mask[:, :, None].astype(jnp.bfloat16)
    first_layer_destinations = cols1 - col_index * col_blocks
    second_targets = cols2 - row_index * row_blocks
    first_offset_value = jnp.zeros((rows_dev, col_blocks, block), jnp.float32)
    first_fold = fold_function(masked, first_layer_destinations, w1.shape[0])
    first_sum = first_fold(
        first_offset_value, lax.all_gather(w1, "depth", axis=0, tiled=True), jnp.int32(0)
    )
    bias_blocks = bias1.reshape(col_blocks, block)
    share = col_blocks // lax.axis_size("row")
    part_sum = lax.psum_scatter(first_sum, "row", scatter_dimension=1, tiled=True)
    bias_part = lax.dynamic_slice_in_dim(bias_blocks, row_index * share, share, 0)
    mask_part = lax.dynamic_slice_in_dim(mask2, row_index * share, share, 1)
    hidden_part = jnp.maximum(part_sum + bias_part, 0.0) * mask_part[:, :, None].astype(jnp.float32)
    hidden = lax.all_gather(hidden_part.astype(jnp.bfloat16), "row", axis=1, tiled=True)
    second_start = jnp.zeros((rows_dev, row_blocks, block), jnp.float32)
    second_fold = fold_function(hidden, second_targets, w2.shape[0])
    second_sum = second_fold(
        second_start, lax.all_gather(w2, "depth", axis=0, tiled=True), jnp.int32(0)
    )
    outcome = lax.psum_scatter(second_sum, "col", scatter_dimension=1, tiled=True)
    bias_out = bias2.reshape(outcome.shape[1], block)
    return jnp.maximum(outcome + bias_out, 0.0).astype(jnp.bfloat16).reshape(rows_dev, -1)


def solution(mesh):
    return jax.shard_map(
        on_device,
        mesh=mesh,
        in_specs=(
            P("depth", "row"),
            P("depth", "row"),
            P(("row", "depth"), "col", None, None),
            P("row", "col"),
            P("col"),
            P("depth", "col"),
            P(("col", "depth"), "row", None, None),
            P("col", "row"),
            P(("row", "col")),
        ),
        out_specs=P("depth", ("row", "col")),
        check_vma=False,
    )
```

profile of v0, /device:TPU:0, one launch (start us, length us, event | category | flops | bytes accessed | tf_op | source)
XLA Modules:
  0.0 906.3 jit_solution(17120707963761237808)
XLA Ops:
  6.5 0.7 all-gather.6.cloned.1.call-update
  7.4 0.7 copy-done.3
  8.1 2.4 copy.36
  10.6 1.7 broadcast_multiply_fusion
  12.3 198.1 %all-gather.6.cloned.1.call-done = bf16[64,8,128,128]{3,2,1,0:T(8,128)(2,1)} async-done(((bf16[32,8,128,128]{3,2,1,0:T(8,128)(2,1)}), bf16[64,8,128,128]{3,2,1,0:T(8,128)(2,1)}) %all-gather.6.cloned.1.call-update) | async-done | bytes 16777232 | tf_op jit(solution)/shard_map/all_gather | solution.py:40
  210.5 2.6 broadcast.65.clone
  213.1 162.2 %while.26 = (s32[]{:T(128)}, f32[128,64,128]{2,0,1:T(8,128)}, s32[64,8]{1,0:T(8,128)S(1)}, bf16[64,8,128,128]{3,2,1,0:T(8,128)(2,1)}, bf16[128,64,128]{0,2,1:T(8...) while((s32[]{:T(128)}, f32[128,64,128]{2,0,1:T(8,128)}, s32[64,8]{1,0:T(8,128)S(1)}, ...), condition=%wide.region_2.0_spmd, body=%wide.region_0.0_spmd.sunk | while | flops 1077936896 | bytes 110108816 | solution.py:22
  213.1 11.5 %fusion.18 = f32[32,8,128,128]{3,2,1,0:T(8,128)} fusion(bf16[64,8,128,128]{3,2,1,0:T(8,128)(2,1)} %get-tuple-element.323, s32[]{:T(128)S(6)} %select_n.58, bf16[128,64,128]{0,2,1:T(8,128)(2,1)S(1)} %get-tuple-element.324), kind=kOutput, calls=%fused_computation.2.clone.1 | convolution fusion | flops 1073741824 | bytes 26215424 | tf_op jit(solution)/shard_map/while/body/eval_jaxpr/tws,wish->twih/dot_general | solution.py:16
  224.6 17.4 %copy.51 = f32[128,256,128]{2,0,1:T(8,128)} copy(f32[128,256,128]{0,2,1:T(8,128)} %bitcast.44) | data formatting | bytes 33554432 | tf_op jit(solution)/shard_map/while/body/eval_jaxpr/reshape | solution.py:19
  242.1 52.0 %scatter_fusion = f32[128,64,128]{2,0,1:T(8,128)} fusion(f32[128,64,128]{2,0,1:T(8,128)} %get-tuple-element.312, s32[256]{0:T(256)S(1)} %bitcast.48, f32[256,128,128]{2,1,0:T(8,128)} %bitcast.42), kind=kCustom, calls=%fused_computation.clone.1 | custom fusion | flops 4194304 | bytes 50332672 | tf_op jit(solution)/shard_map/while/body/eval_jaxpr/scatter-add | solution.py:20
  294.1 11.5 %fusion.18 = f32[32,8,128,128]{3,2,1,0:T(8,128)} fusion(bf16[64,8,128,128]{3,2,1,0:T(8,128)(2,1)} %get-tuple-element.323, s32[]{:T(128)S(6)} %select_n.58, bf16[128,64,128]{0,2,1:T(8,128)(2,1)S(1)} %get-tuple-element.324), kind=kOutput, calls=%fused_computation.2.clone.1 | convolution fusion | flops 1073741824 | bytes 26215424 | tf_op jit(solution)/shard_map/while/body/eval_jaxpr/tws,wish->twih/dot_general | solution.py:16
  305.7 17.4 %copy.51 = f32[128,256,128]{2,0,1:T(8,128)} copy(f32[128,256,128]{0,2,1:T(8,128)} %bitcast.44) | data formatting | bytes 33554432 | tf_op jit(solution)/shard_map/while/body/eval_jaxpr/reshape | solution.py:19
  323.2 52.0 %scatter_fusion = f32[128,64,128]{2,0,1:T(8,128)} fusion(f32[128,64,128]{2,0,1:T(8,128)} %get-tuple-element.312, s32[256]{0:T(256)S(1)} %bitcast.48, f32[256,128,128]{2,1,0:T(8,128)} %bitcast.42), kind=kCustom, calls=%fused_computation.clone.1 | custom fusion | flops 4194304 | bytes 50332672 | tf_op jit(solution)/shard_map/while/body/eval_jaxpr/scatter-add | solution.py:20
  375.2 5.6 copy.39
  381.7 0.7 dynamic-slice_convert_fusion
  382.4 43.1 %reduce-scatter.3.cloned.1.call-done = f32[128,16,128]{0,2,1:T(8,128)} async-done(((f32[128,64,128]{0,2,1:T(8,128)}), f32[128,16,128]{0,2,1:T(8,128)}) %reduce-scatter.3.cloned.1.call-update) | async-done | bytes 1048592 | tf_op jit(solution)/shard_map/reduce_scatter | solution.py:44
  425.4 1.6 multiply_convert_fusion
  427.0 1.0 copy.40
  428.2 197.7 %all-gather.4.cloned.1.call-done = bf16[64,8,128,128]{3,2,1,0:T(8,128)(2,1)} async-done(((bf16[32,8,128,128]{3,2,1,0:T(8,128)(2,1)}), bf16[64,8,128,128]{3,2,1,0:T(8,128)(2,1)}) %all-gather.4.cloned.1.call-update) | async-done | bytes 16777232 | tf_op jit(solution)/shard_map/all_gather | solution.py:52
  625.9 24.0 %all-gather.8.cloned.1.call-done = bf16[128,64,128]{2,0,1:T(8,128)(2,1)} async-done(((bf16[128,16,128]{2,0,1:T(8,128)(2,1)}), bf16[128,64,128]{2,0,1:T(8,128)(2,1)}) %all-gather.8.cloned.1.call-update) | async-done | bytes 2097168 | tf_op jit(solution)/shard_map/all_gather | solution.py:48
  649.9 2.6 broadcast.65
  652.5 162.1 %while.27 = (s32[]{:T(128)}, f32[128,64,128]{2,0,1:T(8,128)}, s32[64,8]{1,0:T(8,128)S(1)}, bf16[64,8,128,128]{3,2,1,0:T(8,128)(2,1)}, bf16[128,64,128]{2,0,1:T(8...) while((s32[]{:T(128)}, f32[128,64,128]{2,0,1:T(8,128)}, s32[64,8]{1,0:T(8,128)S(1)}, ...), condition=%wide.region_6.0_spmd, body=%wide.region_4.0_spmd.sunk | while | flops 1077936896 | bytes 110108816 | solution.py:22
  652.5 11.5 %fusion.21 = f32[32,8,128,128]{3,2,1,0:T(8,128)} fusion(bf16[64,8,128,128]{3,2,1,0:T(8,128)(2,1)} %get-tuple-element.350, s32[]{:T(128)S(6)} %select_n.60, bf16[128,64,128]{2,0,1:T(8,128)(2,1)S(1)} %get-tuple-element.351), kind=kOutput, calls=%fused_computation.9.clone.1 | convolution fusion | flops 1073741824 | bytes 26215424 | tf_op jit(solution)/shard_map/while/body/eval_jaxpr/tws,wish->twih/dot_general | solution.py:16
  664.0 17.4 %copy.52 = f32[128,256,128]{2,0,1:T(8,128)} copy(f32[128,256,128]{0,2,1:T(8,128)} %bitcast.45) | data formatting | bytes 33554432 | tf_op jit(solution)/shard_map/while/body/eval_jaxpr/reshape | solution.py:19
  681.5 52.0 %scatter_fusion.1 = f32[128,64,128]{2,0,1:T(8,128)} fusion(f32[128,64,128]{2,0,1:T(8,128)} %get-tuple-element.339, s32[256]{0:T(256)S(1)} %bitcast.49, f32[256,128,128]{2,1,0:T(8,128)} %bitcast.43), kind=kCustom, calls=%fused_computation.1.clone.1 | custom fusion | flops 4194304 | bytes 50332672 | tf_op jit(solution)/shard_map/while/body/eval_jaxpr/scatter-add | solution.py:20
  733.5 11.5 %fusion.21 = f32[32,8,128,128]{3,2,1,0:T(8,128)} fusion(bf16[64,8,128,128]{3,2,1,0:T(8,128)(2,1)} %get-tuple-element.350, s32[]{:T(128)S(6)} %select_n.60, bf16[128,64,128]{2,0,1:T(8,128)(2,1)S(1)} %get-tuple-element.351), kind=kOutput, calls=%fused_computation.9.clone.1 | convolution fusion | flops 1073741824 | bytes 26215424 | tf_op jit(solution)/shard_map/while/body/eval_jaxpr/tws,wish->twih/dot_general | solution.py:16
  745.1 17.4 %copy.52 = f32[128,256,128]{2,0,1:T(8,128)} copy(f32[128,256,128]{0,2,1:T(8,128)} %bitcast.45) | data formatting | bytes 33554432 | tf_op jit(solution)/shard_map/while/body/eval_jaxpr/reshape | solution.py:19
  762.6 51.9 %scatter_fusion.1 = f32[128,64,128]{2,0,1:T(8,128)} fusion(f32[128,64,128]{2,0,1:T(8,128)} %get-tuple-element.339, s32[256]{0:T(256)S(1)} %bitcast.49, f32[256,128,128]{2,1,0:T(8,128)} %bitcast.43), kind=kCustom, calls=%fused_computation.1.clone.1 | custom fusion | flops 4194304 | bytes 50332672 | tf_op jit(solution)/shard_map/while/body/eval_jaxpr/scatter-add | solution.py:20
  814.6 5.6 copy.42
  820.2 77.0 %reduce-scatter.5.cloned.1.call-done = f32[128,16,128]{0,2,1:T(8,128)} async-done(((f32[128,64,128]{0,2,1:T(8,128)}), f32[128,16,128]{0,2,1:T(8,128)}) %reduce-scatter.5.cloned.1.call-update) | async-done | bytes 1048592 | tf_op jit(solution)/shard_map/reduce_scatter | solution.py:54
  897.2 1.6 maximum_convert_fusion
  898.8 1.0 copy.43
  (42 shorter events, 1.5 us)
Async XLA Ops:
  6.5 375.1 %copy-start = (f32[8192]{0:T(1024)S(1)}, f32[8192]{0:T(1024)}, u32[]{:S(2)}) copy-start(f32[8192]{0:T(1024)} %param.17) | copy-start | bytes 98308
  6.5 0.8 copy-start.6
  6.5 1.6 copy-start.3
  6.5 203.9 %all-gather.6.cloned.1.call-start = ((), (), s32[]{:S(2)}) async-start(), calls=%async_computation.3 | async-start | bytes 25165824 | tf_op jit(solution)/shard_map/all_gather | solution.py:40
  7.3 3.3 copy-start.4
  7.3 418.2 %reduce-scatter.3.cloned.1.call-start = ((), (), s32[]{:S(2)}) async-start(), calls=%async_computation.4 | async-start | bytes 5242880 | tf_op jit(solution)/shard_map/reduce_scatter | solution.py:44
  380.9 47.2 %copy-start.7 = (s32[64,8]{0,1:T(8,128)S(1)}, s32[64,8]{0,1:T(8,128)}, u32[]{:S(2)}) copy-start(s32[64,8]{0,1:T(8,128)} %param.20) | copy-start | bytes 6148
  380.9 245.0 %all-gather.4.cloned.1.call-start = ((), (), s32[]{:S(2)}) async-start(), calls=%async_computation.2 | async-start | bytes 25165824 | tf_op jit(solution)/shard_map/all_gather | solution.py:52
  381.6 268.3 %all-gather.8.cloned.1.call-start = ((), (), s32[]{:S(2)}) async-start(), calls=%async_computation.5 | async-start | bytes 2621440 | tf_op jit(solution)/shard_map/all_gather | solution.py:48
  428.1 469.2 %reduce-scatter.5.cloned.1.call-start = ((), (), s32[]{:S(2)}) async-start(), calls=%async_computation.6 | async-start | bytes 5242880 | tf_op jit(solution)/shard_map/reduce_scatter | solution.py:54
  649.9 2.6 copy-start.2
  814.6 85.3 %copy-start.1 = (f32[8192]{0:T(1024)S(1)}, f32[8192]{0:T(1024)}, u32[]{:S(2)}) copy-start(f32[8192]{0:T(1024)} %param.17) | copy-start | bytes 98308
  820.2 77.1 %copy-start.5 = (f32[2048]{0:T(1024)S(1)}, f32[2048]{0:T(1024)}, u32[]{:S(2)}) copy-start(f32[2048]{0:T(1024)} %param.21) | copy-start | bytes 24580
Sparse Core Ops, SparseCore 0:
  8.9 201.5 all-gather.5
  381.0 44.4 reduce-scatter.2
  427.0 198.8 all-gather.3
  627.3 22.5 all-gather.7
  820.3 76.8 reduce-scatter.4
where the time goes:
time: 910 us; the launch traced here: 906 us
  waiting for transfers between devices  541 us (59%)
  other arithmetic  214 us (24%)
  local copies, waits for them, and re-layouts  91.9 us (10%)
  matrix products  46.1 us (5%)
  between operations  13.2 us (1%)
    scatter-add x4, other arithmetic, advance(): return total.at[:, wanted.reshape(-1)].add(flat_product)  208 us
    all_gather x1, waiting for transfers between devices, on_device(): lax.all_gather(w1, 'depth', axis=0, tiled=True)  198 us
    all_gather x1, waiting for transfers between devices, on_device(): lax.all_gather(w2, 'depth', axis=0, tiled=True)  198 us
    reduce_scatter x1, waiting for transfers between devices, on_device(): lax.psum_scatter(second_sum, 'col', scatter_dimension=1, tiled=True)  77 us
    reshape x4, local copies, waits for them, and re-layouts, advance(): flat_product = product.reshape(product.shape[0], -1, product.shape[-1])  69.7 us
    dot_general x4, matrix products, advance(): jnp.einsum('tws,wish->twih', incoming_rows, block_list, preferred_element...  46.1 us
    reduce_scatter x1, waiting for transfers between devices, on_device(): lax.psum_scatter(first_sum, 'row', scatter_dimension=1, tiled=True)  43.1 us
    all_gather x1, waiting for transfers between devices, on_device(): lax.all_gather(hidden_part.astype(jnp.bfloat16), 'row', axis=1, tiled=True)  24 us
  transfers between devices with their start and end apart: 5, of which 5 were waited for; matrix products, arithmetic and copies ran while one was open for 1% of the time, Pallas kernels for 0%

commit v1 on v0

--- a/solution.py
+++ b/solution.py
@@ -1,6 +1,10 @@
+import functools
+
 import jax
 import jax.numpy as jnp
 from jax import lax
+from jax.experimental import pallas as pl
+from jax.experimental.pallas import tpu as pltpu
 from jax.sharding import PartitionSpec as P
 
 
@@ -24,7 +28,7 @@
     return add_tiles
 
 
-def on_device(acts, act_mask, w1, cols1, bias1, mask2, w2, cols2, bias2):
+def gathered_weights(acts, act_mask, w1, cols1, bias1, mask2, w2, cols2, bias2):
     block = w1.shape[-1]
     rows_dev = acts.shape[0]
     row_blocks = act_mask.shape[1]
@@ -56,9 +60,113 @@
     return jnp.maximum(outcome + bias_out, 0.0).astype(jnp.bfloat16).reshape(rows_dev, -1)
 
 
+def sparse_kernel(per_step, entries, blocked, cols_ref, x_ref, w_ref, out_ref, total):
+    step = pl.program_id(0)
+    block = w_ref.shape[-1]
+
+    @pl.when(step == 0)
+    def _():
+        total[...] = jnp.zeros_like(total)
+
+    for row in range(per_step):
+        if blocked:
+            x = x_ref[row]
+        else:
+            x = x_ref[:, row * block:(row + 1) * block]
+        for entry in range(0, entries, 2):
+            pair = jnp.concatenate([w_ref[row, entry], w_ref[row, entry + 1]], axis=1)
+            product = jnp.dot(x, pair, preferred_element_type=jnp.float32)
+            base = (step * per_step + row) * entries + entry
+            total[cols_ref[base]] += product[:, :block]
+            total[cols_ref[base + 1]] += product[:, block:]
+
+    @pl.when(step == pl.num_programs(0) - 1)
+    def _():
+        out_ref[...] = total[...].astype(out_ref.dtype)
+
+
+def sparse_partial(x, weights, cols, out_blocks, blocked, kind=jnp.float32):
+    stored, entries, block, _ = weights.shape
+    rows = x.shape[1] if blocked else x.shape[0]
+    per_step = 4 if stored % 4 == 0 else 1
+    if blocked:
+        x_spec = pl.BlockSpec((per_step, rows, block), lambda i, c: (i, 0, 0))
+    else:
+        x_spec = pl.BlockSpec((rows, per_step * block), lambda i, c: (0, i))
+    return pl.pallas_call(
+        functools.partial(sparse_kernel, per_step, entries, blocked),
+        out_shape=jax.ShapeDtypeStruct((out_blocks, rows, block), kind),
+        grid_spec=pltpu.PrefetchScalarGridSpec(
+            num_scalar_prefetch=1,
+            grid=(stored // per_step,),
+            in_specs=[
+                x_spec,
+                pl.BlockSpec((per_step, entries, block, block), lambda i, c: (i, 0, 0, 0)),
+            ],
+            out_specs=pl.BlockSpec((out_blocks, rows, block), lambda i, c: (0, 0, 0)),
+            scratch_shapes=[pltpu.VMEM((out_blocks, rows, block), jnp.float32)],
+        ),
+        compiler_params=pltpu.CompilerParams(
+            dimension_semantics=("arbitrary",), vmem_limit_bytes=40 * 1024 * 1024
+        ),
+        cost_estimate=pl.CostEstimate(
+            flops=2 * rows * weights.size, bytes_accessed=2 * weights.size, transcendentals=0
+        ),
+    )(cols.reshape(-1), x, weights)
+
+
+def exchanged_rows(acts, act_mask, w1, cols1, bias1, mask2, w2, cols2, bias2):
+    f32, bf16 = jnp.float32, jnp.bfloat16
+    block = w1.shape[-1]
+    stored1, stored2 = w1.shape[0], w2.shape[0]
+    rows = acts.shape[0]
+    row_blocks, col_blocks = act_mask.shape[1], mask2.shape[1]
+    r, c, d = lax.axis_index("row"), lax.axis_index("col"), lax.axis_index("depth")
+    n_row, n_col = lax.axis_size("row"), lax.axis_size("col")
+    other = 1 - d
+    swap = [(0, 1), (1, 0)]
+    masked = (acts.reshape(rows, row_blocks, block) * act_mask[:, :, None].astype(bf16)).reshape(rows, -1)
+    keep = lax.dynamic_slice_in_dim(masked, d * stored1 * block, stored1 * block, 1)
+    give = lax.dynamic_slice_in_dim(masked, other * stored1 * block, stored1 * block, 1)
+    taken = lax.ppermute(give, "depth", swap)
+    to1 = lax.dynamic_slice_in_dim(cols1, d * stored1, stored1, 0) - c * col_blocks
+    to2 = lax.dynamic_slice_in_dim(cols2, d * stored2, stored2, 0) - r * row_blocks
+    mine = sparse_partial(keep, w1, to1, col_blocks, False)
+    theirs = sparse_partial(taken, w1, to1, col_blocks, False)
+    half = col_blocks // 2
+    sent = jnp.stack([
+        lax.dynamic_slice_in_dim(theirs, other * half, half, 0),
+        lax.dynamic_slice_in_dim(mine, other * half, half, 0),
+    ])
+    held = jnp.stack([
+        lax.dynamic_slice_in_dim(mine, d * half, half, 0),
+        lax.dynamic_slice_in_dim(theirs, d * half, half, 0),
+    ])
+    came = lax.ppermute(sent.astype(bf16), "depth", swap)
+    both = (held + came.astype(f32)).astype(bf16)
+    share = half // n_row
+    spread = lax.all_to_all(both.reshape(2, n_row, share, rows, block), "row", 1, 1)
+    z1 = spread.astype(f32).sum(1)
+    first = d * half + r * share
+    bias_part = lax.dynamic_slice_in_dim(bias1.reshape(col_blocks, block), first, share, 0)
+    live = jnp.stack([mask2, lax.ppermute(mask2.astype(f32), "depth", swap).astype(jnp.int32)])
+    live = lax.dynamic_slice_in_dim(live, first, share, 2).transpose(0, 2, 1)
+    x1 = (jnp.maximum(z1 + bias_part[:, None, :], 0.0) * live[..., None].astype(f32)).astype(bf16)
+    x1 = lax.all_gather(x1, "row", axis=1, tiled=True)
+    away = sparse_partial(x1[1], w2, to2, row_blocks, True, bf16)
+    back = lax.ppermute(away, "depth", swap)
+    home = sparse_partial(x1[0], w2, to2, row_blocks, True)
+    z2 = (home + back.astype(f32)).astype(bf16)
+    out_share = row_blocks // n_col
+    z2 = lax.all_to_all(z2.reshape(n_col, out_share, rows, block), "col", 0, 0)
+    z2 = z2.astype(f32).sum(0)
+    out = jnp.maximum(z2 + bias2.reshape(out_share, 1, block), 0.0).astype(bf16)
+    return out.transpose(1, 0, 2).reshape(rows, -1)
+
+
 def solution(mesh):
     return jax.shard_map(
-        on_device,
+        exchanged_rows if mesh.shape["depth"] == 2 else gathered_weights,
         mesh=mesh,
         in_specs=(
             P("depth", "row"),

time: 910 us -> 269 us (0.30)
  waiting for transfers between devices: 541 us -> 144 us
  other arithmetic: 214 us -> 5.97 us
  local copies, waits for them, and re-layouts: 91.9 us -> 21.5 us
  blocking collectives: 0 us -> 52.1 us
  matrix products: 46.1 us -> 0 us
  Pallas kernels: 0 us -> 19.3 us
  starting transfers between devices: 0.16 us -> 11.7 us
    all_gather x3 -> x1, waiting for transfers between devices: 420 us -> 22.8 us  [exchanged_rows(): x1 = lax.all_gather(x1, 'row', axis=1, tiled=True)]
    scatter-add x4 -> x0, other arithmetic: 208 us -> none  [advance(): return total.at[:, wanted.reshape(-1)].add(flat_product)]
    reduce_scatter x2 -> x0, waiting for transfers between devices: 120 us -> none  [the longest x1 77 us: on_device(): lax.psum_scatter(second_sum, 'col', scatter_dimension=1, tiled=True)]
    ppermute x0 -> x4, waiting for transfers between devices: none -> 99.6 us  [the longest x1 44.6 us: exchanged_rows(): came = lax.ppermute(sent.astype(bf16), 'depth', swap)]
    reshape x9 -> x4, local copies, waits for them, and re-layouts: 71.1 us -> 2.77 us  [the longest x1 1.58 us: exchanged_rows(): both.reshape(2, n_row, share, rows, block)]
    all_to_all x0 -> x1, blocking collectives: none -> 52.1 us  [exchanged_rows(): z2 = lax.all_to_all(z2.reshape(n_col, out_share, rows, block), 'col', 0, 0)]
    dot_general x4 -> x0, matrix products: 46.1 us -> none  [advance(): jnp.einsum('tws,wish->twih', incoming_rows, block_list, preferred_element...]
    all_to_all x0 -> x1, waiting for transfers between devices: none -> 21.6 us  [exchanged_rows(): lax.all_to_all(both.reshape(2, n_row, share, rows, block), 'row', 1, 1)]
  transfers between devices with their start and end apart: 5 -> 6, of which waited for: 5 -> 6; matrix products, arithmetic and copies ran while one was open for 1% -> 0% of each run, Pallas kernels for 0% -> 4%
where the time goes in v1:
time: 269 us; the launch traced here: 268 us
  waiting for transfers between devices  144 us (54%)
  blocking collectives  52.1 us (19%)
  local copies, waits for them, and re-layouts  21.5 us (8%)
  Pallas kernels  19.3 us (7%)
  between operations  13.6 us (5%)
  starting transfers between devices  11.7 us (4%)
  other arithmetic  5.97 us (2%)
    all_to_all x1, blocking collectives, exchanged_rows(): z2 = lax.all_to_all(z2.reshape(n_col, out_share, rows, block), 'col', 0, 0)  52.1 us
    ppermute x1, waiting for transfers between devices, exchanged_rows(): came = lax.ppermute(sent.astype(bf16), 'depth', swap)  44.6 us
    ppermute x1, waiting for transfers between devices, exchanged_rows(): back = lax.ppermute(away, 'depth', swap)  38.1 us
    all_gather x1, waiting for transfers between devices, exchanged_rows(): x1 = lax.all_gather(x1, 'row', axis=1, tiled=True)  22.8 us
    all_to_all x1, waiting for transfers between devices, exchanged_rows(): lax.all_to_all(both.reshape(2, n_row, share, rows, block), 'row', 1, 1)  21.6 us
    pallas_call x4, Pallas kernels, sparse_partial(): pl.pallas_call(functools.partial(sparse_kernel, per_step, entries, blocke...  19.3 us
    ppermute x1, waiting for transfers between devices, exchanged_rows(): taken = lax.ppermute(give, 'depth', swap)  14.4 us
    unnamed x20, local copies, waits for them, and re-layouts  13.9 us
  transfers between devices with their start and end apart: 6, of which 6 were waited for; matrix products, arithmetic and copies ran while one was open for 0% of the time, Pallas kernels for 4%

profile of v1, /device:TPU:0, one launch (start us, length us, event | category | flops | bytes accessed | tf_op | source)
XLA Modules:
  0.0 268.3 jit_solution(10823893698223197385)
XLA Ops:
  6.5 0.9 convert_element_type.46
  7.6 1.6 mul.50
  9.2 1.3 bitcast_multiply_fusion
  10.7 3.1 %collective-permute-start = (bf16[128,4096]{1,0:T(8,128)(2,1)S(1)}, bf16[128,4096]{1,0:T(8,128)(2,1)S(1)}, u32[]{:S(2)}, u32[]{:S(2)}) collective-permute-start(bf16[128,4096]{1,0:T(8,128)(2,1)S(1)} %get-tuple-element.8), channel_id=1, source_target_pairs={{0,1},{1,0},{2,3},{3,2},{4,5},{5,4},{6,7},{7,6},{8,9},{9,8},{10,11... | collective-permute-start | bytes 3145736 | tf_op jit(solution)/shard_map/ppermute | solution.py:131
  14.1 3.4 %copy-done.1 = bf16[32,8,128,128]{3,2,1,0:T(8,128)(2,1)S(1)} copy-done((bf16[32,8,128,128]{3,2,1,0:T(8,128)(2,1)S(1)}, bf16[32,8,128,128]{3,2,1,0:T(8,128)(2,1)}, u32[]{:S(2)}) %copy-start.1) | copy-done | bytes 8388632
  17.4 4.9 %shard_map.91 = f32[64,128,128]{2,1,0:T(8,128)S(1)} custom-call(s32[256]{0:T(256)S(1)} %reshape.31.cols_ref, bf16[128,4096]{1,0:T(8,128)(2,1)S(1)} %get-tuple-element.7.x_ref, bf16[32,8,128,128]{3,2,1,0:T(8,128)(2,1)S(1)} %copy-done.1), custom_call_target="tpu_custom_call" | custom-call | flops 1073741824 | bytes 8388608 | tf_op jit(solution)/shard_map/pallas_call | solution.py:96
  22.5 14.4 %collective-permute-done.x_ref = bf16[128,4096]{1,0:T(8,128)(2,1)S(1)} collective-permute-done((bf16[128,4096]{1,0:T(8,128)(2,1)S(1)}, bf16[128,4096]{1,0:T(8,128)(2,1)S(1)}, u32[]{:S(2)}, u32[]{:S(2)}) %collective-permute-start) | collective-permute-done | bytes 1048608 | tf_op jit(solution)/shard_map/ppermute | solution.py:131
  37.0 3.4 %copy-done.2 = bf16[32,8,128,128]{3,2,1,0:T(8,128)(2,1)S(1)} copy-done((bf16[32,8,128,128]{3,2,1,0:T(8,128)(2,1)S(1)}, bf16[32,8,128,128]{3,2,1,0:T(8,128)(2,1)}, u32[]{:S(2)}) %copy-start.2) | copy-done | bytes 8388632
  40.3 4.9 %shard_map.92 = f32[64,128,128]{2,1,0:T(8,128)S(1)} custom-call(s32[256]{0:T(256)S(1)} %reshape.31.cols_ref, bf16[128,4096]{1,0:T(8,128)(2,1)S(1)} %collective-permute-done.x_ref, bf16[32,8,128,128]{3,2,1,0:T(8,128)(2,1)S(1)} %copy-done.2), custom_call_target="tpu_custom_call" | custom-call | flops 1073741824 | bytes 8388608 | tf_op jit(solution)/shard_map/pallas_call | solution.py:96
  45.6 1.8 collective-permute-start.1
  47.9 44.6 %collective-permute-done.1 = bf16[2,32,128,128]{3,2,1,0:T(8,128)(2,1)S(1)} collective-permute-done((bf16[2,32,128,128]{3,2,1,0:T(8,128)(2,1)S(1)}, bf16[2,32,128,128]{3,2,1,0:T(8,128)(2,1)S(1)}, u32[]{:S(2)}, u32[]{:S(2)}) %collective-permute-start.1) | collective-permute-done | bytes 2097184 | tf_op jit(solution)/shard_map/ppermute | solution.py:145
  92.5 0.8 fusion
  93.3 1.6 copy.21
  94.9 3.7 %all-to-all-start = ((bf16[2,4,8,128,128]{4,3,2,0,1:T(8,128)(2,1)}), bf16[2,4,8,128,128]{4,3,2,0,1:T(8,128)(2,1)S(1)}, u32[]{:S(2)}, u32[]{:S(2)}) async-start(bf16[2,4,8,128,128]{4,3,2,0,1:T(8,128)(2,1)} %copy.21), calls=%async_computation | async-start | bytes 4194304 | tf_op jit(solution)/shard_map/all_to_all | solution.py:148
  98.7 1.5 collective-permute-start.2
  100.3 2.4 collective-permute-done.2
  102.7 21.6 %all-to-all-done = bf16[2,4,8,128,128]{4,3,2,0,1:T(8,128)(2,1)S(1)} async-done(((bf16[2,4,8,128,128]{4,3,2,0,1:T(8,128)(2,1)}), bf16[2,4,8,128,128]{4,3,2,0,1:T(8,128)(2,1)S(1)}, u32[]{:S(2)}, u32[]{:S(2)}) %all-to-all-start) | async-done | bytes 2097184 | tf_op jit(solution)/shard_map/all_to_all | solution.py:148
  124.3 0.4 convert_reduce_fusion.1
  124.7 1.1 multiply_convert_fusion
  126.0 22.8 %all-gather.2.cloned.1.call-done = bf16[2,32,128,128]{3,2,1,0:T(8,128)(2,1)} async-done(((bf16[2,8,128,128]{3,2,1,0:T(8,128)(2,1)}), bf16[2,32,128,128]{3,2,1,0:T(8,128)(2,1)}) %all-gather.2.cloned.1.call-update) | async-done | bytes 2097168 | tf_op jit(solution)/shard_map/all_gather | solution.py:155
  148.8 1.8 slice_bitcast_fusion
  150.6 3.4 %copy-done.3 = bf16[32,8,128,128]{3,2,1,0:T(8,128)(2,1)S(1)} copy-done((bf16[32,8,128,128]{3,2,1,0:T(8,128)(2,1)S(1)}, bf16[32,8,128,128]{3,2,1,0:T(8,128)(2,1)}, u32[]{:S(2)}) %copy-start.3) | copy-done | bytes 8388632
  154.0 4.7 %shard_map.94 = bf16[64,128,128]{2,1,0:T(8,128)(2,1)S(1)} custom-call(s32[256]{0:T(256)S(1)} %reshape.30.cols_ref, bf16[32,128,128]{2,1,0:T(8,128)(2,1)S(1)} %get-tuple-element.5.x_ref, bf16[32,8,128,128]{3,2,1,0:T(8,128)(2,1)S(1)} %copy-done.3), custom_call_target="tpu_custom_call" | custom-call | flops 1073741824 | bytes 8388608 | tf_op jit(solution)/shard_map/pallas_call | solution.py:96
  158.7 1.5 collective-permute-start.3
  160.3 3.4 %copy-done.4 = bf16[32,8,128,128]{3,2,1,0:T(8,128)(2,1)S(1)} copy-done((bf16[32,8,128,128]{3,2,1,0:T(8,128)(2,1)S(1)}, bf16[32,8,128,128]{3,2,1,0:T(8,128)(2,1)}, u32[]{:S(2)}) %copy-start.4) | copy-done | bytes 8388632
  163.6 4.8 %shard_map.93 = f32[64,128,128]{2,1,0:T(8,128)S(1)} custom-call(s32[256]{0:T(256)S(1)} %reshape.30.cols_ref, bf16[32,128,128]{2,1,0:T(8,128)(2,1)S(1)} %get-tuple-element.6.x_ref, bf16[32,8,128,128]{3,2,1,0:T(8,128)(2,1)S(1)} %copy-done.4), custom_call_target="tpu_custom_call" | custom-call | flops 1073741824 | bytes 8388608 | tf_op jit(solution)/shard_map/pallas_call | solution.py:96
  168.4 38.1 %collective-permute-done.3 = bf16[64,128,128]{2,1,0:T(8,128)(2,1)S(1)} collective-permute-done((bf16[64,128,128]{2,1,0:T(8,128)(2,1)S(1)}, bf16[64,128,128]{2,1,0:T(8,128)(2,1)S(1)}, u32[]{:S(2)}, u32[]{:S(2)}) %collective-permute-start.3) | collective-permute-done | bytes 2097184 | tf_op jit(solution)/shard_map/ppermute | solution.py:157
  206.5 0.7 add_convert_fusion
  207.2 52.1 %all_to_all.10 = bf16[4,16,128,128]{3,2,1,0:T(8,128)(2,1)S(1)} all-to-all(bf16[4,16,128,128]{3,2,1,0:T(8,128)(2,1)S(1)} %bitcast.30), channel_id=1, replica_groups=mesh['row'=4,'col'=4,'depth'=2] {'col'}, dimensions={0} | all-to-all | bytes 4194304 | tf_op jit(solution)/shard_map/all_to_all | solution.py:161
  259.3 0.4 convert_reduce_fusion
  259.7 0.3 copy-done.7
  260.5 1.0 copy.23
  (35 shorter events, 2.2 us)
Async XLA Ops:
  6.5 93.7 %copy-start = (f32[8192]{0:T(1024)S(1)}, f32[8192]{0:T(1024)}, u32[]{:S(2)}) copy-start(f32[8192]{0:T(1024)} %param.13) | copy-start | bytes 98308
  6.5 2.7 copy-start.5
  10.5 3.3 %copy-start.8 = (s32[64,8]{0,1:T(8,128)S(1)}, s32[64,8]{0,1:T(8,128)}, u32[]{:S(2)}) copy-start(s32[64,8]{0,1:T(8,128)} %param.12) | copy-start | bytes 6148
  10.5 3.3 %copy-start.9 = (s32[64,8]{0,1:T(8,128)S(1)}, s32[64,8]{0,1:T(8,128)}, u32[]{:S(2)}) copy-start(s32[64,8]{0,1:T(8,128)} %param.16) | copy-start | bytes 6148
  10.7 26.2 %collective-permute-start = (bf16[128,4096]{1,0:T(8,128)(2,1)S(1)}, bf16[128,4096]{1,0:T(8,128)(2,1)S(1)}, u32[]{:S(2)}, u32[]{:S(2)}) collective-permute-start(bf16[128,4096]{1,0:T(8,128)(2,1)S(1)} %get-tuple-element.8), channel_id=1, source_target_pairs={{0,1},{1,0},{2,3},{3,2},{4,5},{5,4},{6,7},{7,6},{8,9},{9,8},{10,11... | collective-permute-start | bytes 3145736 | tf_op jit(solution)/shard_map/ppermute | solution.py:131
  14.0 3.4 %copy-start.1 = (bf16[32,8,128,128]{3,2,1,0:T(8,128)(2,1)S(1)}, bf16[32,8,128,128]{3,2,1,0:T(8,128)(2,1)}, u32[]{:S(2)}) copy-start(bf16[32,8,128,128]{3,2,1,0:T(8,128)(2,1)} %w_ref.5) | copy-start | bytes 25165828
  37.0 3.4 %copy-start.2 = (bf16[32,8,128,128]{3,2,1,0:T(8,128)(2,1)S(1)}, bf16[32,8,128,128]{3,2,1,0:T(8,128)(2,1)}, u32[]{:S(2)}) copy-start(bf16[32,8,128,128]{3,2,1,0:T(8,128)(2,1)} %w_ref.5) | copy-start | bytes 25165828
  45.6 46.9 %collective-permute-start.1 = (bf16[2,32,128,128]{3,2,1,0:T(8,128)(2,1)S(1)}, bf16[2,32,128,128]{3,2,1,0:T(8,128)(2,1)S(1)}, u32[]{:S(2)}, u32[]{:S(2)}) collective-permute-start(bf16[2,32,128,128]{3,2,1,0:T(8,128)(2,1)S(1)} %pad_maximum_fusion), channel_id=1, source_target_pairs={{0,1},{1,0},{2,3},{3,2},{4,5},{5,4},{6,7},{7,6},{8,9},{9,8},{10,11... | collective-permute-start | bytes 6291464 | tf_op jit(solution)/shard_map/ppermute | solution.py:145
  94.9 3.8 %copy-start.6 = (s32[128,64]{0,1:T(8,128)S(1)}, s32[128,64]{0,1:T(8,128)}, u32[]{:S(2)}) copy-start(s32[128,64]{0,1:T(8,128)} %param.14) | copy-start | bytes 98308
  94.9 29.4 %all-to-all-start = ((bf16[2,4,8,128,128]{4,3,2,0,1:T(8,128)(2,1)}), bf16[2,4,8,128,128]{4,3,2,0,1:T(8,128)(2,1)S(1)}, u32[]{:S(2)}, u32[]{:S(2)}) async-start(bf16[2,4,8,128,128]{4,3,2,0,1:T(8,128)(2,1)} %copy.21), calls=%async_computation | async-start | bytes 4194304 | tf_op jit(solution)/shard_map/all_to_all | solution.py:148
  98.7 50.2 %all-gather.2.cloned.1.call-start = ((), (), s32[]{:S(2)}) async-start(), calls=%async_computation.2 | async-start | bytes 2621440 | tf_op jit(solution)/shard_map/all_gather | solution.py:155
  98.7 4.0 %collective-permute-start.2 = (f32[128,64]{0,1:T(8,128)S(1)}, f32[128,64]{0,1:T(8,128)S(1)}, u32[]{:S(2)}, u32[]{:S(2)}) collective-permute-start(f32[128,64]{0,1:T(8,128)S(1)} %convert_element_type.50), channel_id=1, source_target_pairs={{0,1},{1,0},{2,3},{3,2},{4,5},{5,4},{6,7},{7,6},{8,9},{9,8},{10,11... | collective-permute-start | bytes 98312 | tf_op jit(solution)/shard_map/ppermute | solution.py:152
  150.6 3.4 %copy-start.3 = (bf16[32,8,128,128]{3,2,1,0:T(8,128)(2,1)S(1)}, bf16[32,8,128,128]{3,2,1,0:T(8,128)(2,1)}, u32[]{:S(2)}) copy-start(bf16[32,8,128,128]{3,2,1,0:T(8,128)(2,1)} %w_ref.7) | copy-start | bytes 25165828
  158.7 47.8 %collective-permute-start.3 = (bf16[64,128,128]{2,1,0:T(8,128)(2,1)S(1)}, bf16[64,128,128]{2,1,0:T(8,128)(2,1)S(1)}, u32[]{:S(2)}, u32[]{:S(2)}) collective-permute-start(bf16[64,128,128]{2,1,0:T(8,128)(2,1)S(1)} %shard_map.94), channel_id=1, source_target_pairs={{0,1},{1,0},{2,3},{3,2},{4,5},{5,4},{6,7},{7,6},{8,9},{9,8},{10,11... | collective-permute-start | bytes 6291464 | tf_op jit(solution)/shard_map/ppermute | solution.py:157
  160.3 3.4 %copy-start.4 = (bf16[32,8,128,128]{3,2,1,0:T(8,128)(2,1)S(1)}, bf16[32,8,128,128]{3,2,1,0:T(8,128)(2,1)}, u32[]{:S(2)}) copy-start(bf16[32,8,128,128]{3,2,1,0:T(8,128)(2,1)} %w_ref.7) | copy-start | bytes 25165828
  259.3 0.7 copy-start.7
Sparse Core Ops, SparseCore 0:
  126.0 22.8 all-gather.1

commit v2 on v1

--- a/solution.py
+++ b/solution.py
@@ -60,7 +60,8 @@
     return jnp.maximum(outcome + bias_out, 0.0).astype(jnp.bfloat16).reshape(rows_dev, -1)
 
 
-def sparse_kernel(per_step, entries, blocked, cols_ref, x_ref, w_ref, out_ref, total):
+def sparse_kernel(per_step, entries, blocked, cols_ref, core_ref, x_ref, w_ref, *refs):
+    *outs, total = refs
     step = pl.program_id(0)
     block = w_ref.shape[-1]
 
@@ -82,28 +83,38 @@
 
     @pl.when(step == pl.num_programs(0) - 1)
     def _():
-        out_ref[...] = total[...].astype(out_ref.dtype)
-
-
-def sparse_partial(x, weights, cols, out_blocks, blocked, kind=jnp.float32):
+        if len(outs) == 1:
+            outs[0][...] = total[...].astype(outs[0].dtype)
+        else:
+            kept, given = outs
+            pieces, size = kept.shape[:2]
+            core = core_ref[0]
+            for piece in range(pieces):
+                start = piece * 2 * size
+                kept[piece] = total[pl.ds(start + core * size, size)]
+                given[piece] = total[pl.ds(start + (1 - core) * size, size)].astype(given.dtype)
+
+
+def sparse_partial(x, weights, cols, core, out_blocks, blocked, outs):
     stored, entries, block, _ = weights.shape
     rows = x.shape[1] if blocked else x.shape[0]
     per_step = 4 if stored % 4 == 0 else 1
     if blocked:
-        x_spec = pl.BlockSpec((per_step, rows, block), lambda i, c: (i, 0, 0))
+        x_spec = pl.BlockSpec((per_step, rows, block), lambda i, *_: (i, 0, 0))
     else:
-        x_spec = pl.BlockSpec((rows, per_step * block), lambda i, c: (0, i))
+        x_spec = pl.BlockSpec((rows, per_step * block), lambda i, *_: (0, i))
+    zeros = [(lambda n: lambda i, *_: (0,) * n)(len(out.shape)) for out in outs]
     return pl.pallas_call(
         functools.partial(sparse_kernel, per_step, entries, blocked),
-        out_shape=jax.ShapeDtypeStruct((out_blocks, rows, block), kind),
+        out_shape=outs,
         grid_spec=pltpu.PrefetchScalarGridSpec(
-            num_scalar_prefetch=1,
+            num_scalar_prefetch=2,
             grid=(stored // per_step,),
             in_specs=[
                 x_spec,
-                pl.BlockSpec((per_step, entries, block, block), lambda i, c: (i, 0, 0, 0)),
+                pl.BlockSpec((per_step, entries, block, block), lambda i, *_: (i, 0, 0, 0)),
             ],
-            out_specs=pl.BlockSpec((out_blocks, rows, block), lambda i, c: (0, 0, 0)),
+            out_specs=[pl.BlockSpec(out.shape, zero) for out, zero in zip(outs, zeros)],
             scratch_shapes=[pltpu.VMEM((out_blocks, rows, block), jnp.float32)],
         ),
         compiler_params=pltpu.CompilerParams(
@@ -112,11 +123,225 @@
         cost_estimate=pl.CostEstimate(
             flops=2 * rows * weights.size, bytes_accessed=2 * weights.size, transcendentals=0
         ),
-    )(cols.reshape(-1), x, weights)
+    )(cols.reshape(-1), core.reshape(1), x, weights)
+
+
+MESH = pl.DeviceIdType.MESH
+F32, BF16 = jnp.float32, jnp.bfloat16
+
+
+def greet(partners):
+    barrier = pltpu.get_barrier_semaphore()
+    for partner in partners:
+        pl.semaphore_signal(barrier, inc=1, device_id=partner, device_id_type=MESH)
+    pl.semaphore_wait(barrier, len(partners))
+
+
+def first_reduce_kernel(
+    chunks, kept0, kept1, given0, given1, bias, live, out,
+    core_in, total, y_out, y_in, x_out, x_in, send_sem, recv_sem,
+):
+    r, d = lax.axis_index("row"), lax.axis_index("depth")
+    x, core = r // 2, r % 2
+    partner = {"row": x * 2 + 1 - core}
+    y_peer = {"depth": 1 - d}
+    x_peer = {"row": (1 - x) * 2 + core}
+    kept, given = (kept0, kept1), (given0, given1)
+    size = kept0.shape[2] // chunks
+    steps = [(half, part) for part in range(chunks) for half in range(2)]
+    arrivals = [(1 - half, part) for half, part in steps]
+    started = []
+
+    def send(stage, source, target, step, landing, device):
+        copy = pltpu.make_async_remote_copy(
+            src_ref=source, dst_ref=target,
+            send_sem=send_sem.at[stage, step[0], step[1]],
+            recv_sem=recv_sem.at[stage, landing[0], landing[1]],
+            device_id=device, device_id_type=MESH,
+        )
+        copy.start()
+        started.append(copy)
+
+    def await_arrival(stage, target, step):
+        pltpu.make_async_remote_copy(
+            src_ref=target, dst_ref=target,
+            send_sem=send_sem.at[stage, step[0], step[1]],
+            recv_sem=recv_sem.at[stage, step[0], step[1]],
+            device_id=x_peer, device_id_type=MESH,
+        ).wait_recv()
+
+    greet([partner, y_peer, x_peer])
+    for step in steps:
+        half, part = step
+        cut = pl.ds(part * size, size)
+        send(0, given[half].at[:, :, cut], core_in.at[half, part], step, step, partner)
+
+    def pair(step):
+        half, part = step
+        cut = pl.ds(part * size, size)
+        await_arrival(0, core_in.at[half, part], step)
+        y_out[half, part] = (
+            kept[half][1 - d, :, cut] + core_in[half, part, 1 - d].astype(F32)
+        ).astype(BF16)
+        send(1, y_out.at[half, part], y_in.at[1 - half, part], step, (1 - half, part), y_peer)
+        total[half, part] = kept[half][d, :, cut] + core_in[half, part, d].astype(F32)
+
+    def along_y(step):
+        half, part = step
+        await_arrival(1, y_in.at[half, part], step)
+        x_out[half, part] = (
+            total[half, part, 1 - x] + y_in[half, part, 1 - x].astype(F32)
+        ).astype(BF16)
+        send(2, x_out.at[half, part], x_in.at[half, part], step, step, x_peer)
+
+    def along_x(step):
+        half, part = step
+        cut = pl.ds(part * size, size)
+        await_arrival(2, x_in.at[half, part], step)
+        z = total[half, part, x] + y_in[half, part, x].astype(F32) + x_in[half, part].astype(F32)
+        for b in range(size):
+            at = part * size + b
+            value = jnp.maximum(z[b] + bias[at:at + 1, :], 0.0) * live[half, :, at:at + 1]
+            out[half, x, core, at] = value.astype(BF16)
+        mine = out.at[half, x, core, cut]
+        send(3, mine, mine, step, step, x_peer)
+        send(4, mine, mine, step, step, partner)
+
+    def forward(step):
+        half, part = step
+        cut = pl.ds(part * size, size)
+        await_arrival(3, out.at[half, 1 - x, core, cut], step)
+        theirs = out.at[half, 1 - x, core, cut]
+        send(5, theirs, theirs, step, step, partner)
+
+    count = len(steps)
+    for at in range(count + 3):
+        if at < count:
+            pair(steps[at])
+        if 0 <= at - 1 < count:
+            along_y(arrivals[at - 1])
+        if 0 <= at - 2 < count:
+            along_x(arrivals[at - 2])
+        if 0 <= at - 3 < count:
+            forward(arrivals[at - 3])
+    for step in arrivals:
+        half, part = step
+        cut = pl.ds(part * size, size)
+        await_arrival(4, out.at[half, x, 1 - core, cut], step)
+        await_arrival(5, out.at[half, 1 - x, 1 - core, cut], step)
+    for copy in started:
+        copy.wait_send()
+
+
+def first_reduce(kept, given, bias, live):
+    _, _, share, rows, block = kept[0].shape
+    chunks = 2 if share % 2 == 0 else 1
+    size = share // chunks
+    vmem = pl.BlockSpec(memory_space=pltpu.VMEM)
+    return pl.pallas_call(
+        functools.partial(first_reduce_kernel, chunks),
+        out_shape=jax.ShapeDtypeStruct((2, 2, 2, share, rows, block), BF16),
+        in_specs=[vmem] * 6,
+        out_specs=vmem,
+        scratch_shapes=[
+            pltpu.VMEM((2, chunks, 2, 2, size, rows, block), BF16),
+            pltpu.VMEM((2, chunks, 2, size, rows, block), F32),
+            pltpu.VMEM((2, chunks, 2, size, rows, block), BF16),
+            pltpu.VMEM((2, chunks, 2, size, rows, block), BF16),
+            pltpu.VMEM((2, chunks, size, rows, block), BF16),
+            pltpu.VMEM((2, chunks, size, rows, block), BF16),
+            pltpu.SemaphoreType.DMA((6, 2, chunks)),
+            pltpu.SemaphoreType.DMA((6, 2, chunks)),
+        ],
+        compiler_params=pltpu.CompilerParams(
+            collective_id=1, has_side_effects=True, vmem_limit_bytes=48 * 1024 * 1024
+        ),
+        name="first_reduce",
+    )(*kept, *given, bias, live)
+
+
+def second_reduce_kernel(n_col, parts, home, away, bias, out, y_in, z_out, z_in, send_y, recv_y, send_z, recv_z):
+    c, d = lax.axis_index("col"), lax.axis_index("depth")
+    share, block = out.shape[1] // home.shape[2], home.shape[2]
+    size = home.shape[1] // parts
+    y_peer = {"depth": 1 - d}
+    offsets = sorted(range(1, n_col), key=lambda o: -min(o, n_col - o)) + [0]
+    steps = [(o, p) for o in offsets for p in range(parts)]
+
+    def target(o):
+        return lax.rem(c + o, n_col)
+
+    def y_copy(o, p):
+        return pltpu.make_async_remote_copy(
+            src_ref=away.at[pl.ds(target(o) * share, share), pl.ds(p * size, size)],
+            dst_ref=y_in.at[o, p],
+            send_sem=send_y.at[o, p], recv_sem=recv_y.at[o, p],
+            device_id=y_peer, device_id_type=MESH,
+        )
+
+    def z_copy(o, p):
+        return pltpu.make_async_remote_copy(
+            src_ref=z_out.at[o - 1, p], dst_ref=z_in.at[o - 1, p],
+            send_sem=send_z.at[o - 1, p], recv_sem=recv_z.at[o - 1, p],
+            device_id={"col": target(o)}, device_id_type=MESH,
+        )
+
+    greet([y_peer] + [{"col": target(o)} for o in range(1, n_col)])
+    for o, p in steps:
+        y_copy(o, p).start()
+    for o, p in steps:
+        if o == 0:
+            continue
+        y_copy(o, p).wait_recv()
+        z_out[o - 1, p] = (
+            home[pl.ds(target(o) * share, share), p * size:(p + 1) * size]
+            + y_in[o, p].astype(F32)
+        ).astype(BF16)
+        z_copy(o, p).start()
+    for p in range(parts):
+        y_copy(0, p).wait_recv()
+        for o in range(1, n_col):
+            z_copy(o, p).wait_recv()
+        for b in range(share):
+            value = home[c * share + b, p * size:(p + 1) * size] + y_in[0, p, b].astype(F32)
+            for o in range(1, n_col):
+                value += z_in[o - 1, p, b].astype(F32)
+            value = jnp.maximum(value + bias[b:b + 1, :], 0.0)
+            out[p * size:(p + 1) * size, b * block:(b + 1) * block] = value.astype(BF16)
+    for o, p in steps:
+        y_copy(o, p).wait_send()
+        if o:
+            z_copy(o, p).wait_send()
+
+
+def second_reduce(home, away, bias, n_col):
+    blocks, rows, block = home.shape
+    share = blocks // n_col
+    parts = 2
+    size = rows // parts
+    vmem = pl.BlockSpec(memory_space=pltpu.VMEM)
+    return pl.pallas_call(
+        functools.partial(second_reduce_kernel, n_col, parts),
+        out_shape=jax.ShapeDtypeStruct((rows, share * block), BF16),
+        in_specs=[vmem] * 3,
+        out_specs=vmem,
+        scratch_shapes=[
+            pltpu.VMEM((n_col, parts, share, size, block), BF16),
+            pltpu.VMEM((n_col - 1, parts, share, size, block), BF16),
+            pltpu.VMEM((n_col - 1, parts, share, size, block), BF16),
+            pltpu.SemaphoreType.DMA((n_col, parts)),
+            pltpu.SemaphoreType.DMA((n_col, parts)),
+            pltpu.SemaphoreType.DMA((n_col - 1, parts)),
+            pltpu.SemaphoreType.DMA((n_col - 1, parts)),
+        ],
+        compiler_params=pltpu.CompilerParams(
+            collective_id=2, has_side_effects=True, vmem_limit_bytes=48 * 1024 * 1024
+        ),
+        name="second_reduce",
+    )(home, away, bias)
 
 
 def exchanged_rows(acts, act_mask, w1, cols1, bias1, mask2, w2, cols2, bias2):
-    f32, bf16 = jnp.float32, jnp.bfloat16
     block = w1.shape[-1]
     stored1, stored2 = w1.shape[0], w2.shape[0]
     rows = acts.shape[0]
@@ -125,48 +350,38 @@
     n_row, n_col = lax.axis_size("row"), lax.axis_size("col")
     other = 1 - d
     swap = [(0, 1), (1, 0)]
-    masked = (acts.reshape(rows, row_blocks, block) * act_mask[:, :, None].astype(bf16)).reshape(rows, -1)
+    masked = (acts.reshape(rows, row_blocks, block) * act_mask[:, :, None].astype(BF16)).reshape(rows, -1)
     keep = lax.dynamic_slice_in_dim(masked, d * stored1 * block, stored1 * block, 1)
     give = lax.dynamic_slice_in_dim(masked, other * stored1 * block, stored1 * block, 1)
     taken = lax.ppermute(give, "depth", swap)
     to1 = lax.dynamic_slice_in_dim(cols1, d * stored1, stored1, 0) - c * col_blocks
     to2 = lax.dynamic_slice_in_dim(cols2, d * stored2, stored2, 0) - r * row_blocks
-    mine = sparse_partial(keep, w1, to1, col_blocks, False)
-    theirs = sparse_partial(taken, w1, to1, col_blocks, False)
-    half = col_blocks // 2
-    sent = jnp.stack([
-        lax.dynamic_slice_in_dim(theirs, other * half, half, 0),
-        lax.dynamic_slice_in_dim(mine, other * half, half, 0),
-    ])
-    held = jnp.stack([
-        lax.dynamic_slice_in_dim(mine, d * half, half, 0),
-        lax.dynamic_slice_in_dim(theirs, d * half, half, 0),
-    ])
-    came = lax.ppermute(sent.astype(bf16), "depth", swap)
-    both = (held + came.astype(f32)).astype(bf16)
-    share = half // n_row
-    spread = lax.all_to_all(both.reshape(2, n_row, share, rows, block), "row", 1, 1)
-    z1 = spread.astype(f32).sum(1)
-    first = d * half + r * share
+    core = r % 2
+    share = col_blocks // 2 // n_row
+    shape1 = (col_blocks // share // 2, share, rows, block)
+    outs1 = [jax.ShapeDtypeStruct(shape1, F32), jax.ShapeDtypeStruct(shape1, BF16)]
+    kept0, given0 = sparse_partial(keep, w1, to1, core, col_blocks, False, outs1)
+    kept1, given1 = sparse_partial(taken, w1, to1, core, col_blocks, False, outs1)
+    first = d * (col_blocks // 2) + r * share
     bias_part = lax.dynamic_slice_in_dim(bias1.reshape(col_blocks, block), first, share, 0)
-    live = jnp.stack([mask2, lax.ppermute(mask2.astype(f32), "depth", swap).astype(jnp.int32)])
-    live = lax.dynamic_slice_in_dim(live, first, share, 2).transpose(0, 2, 1)
-    x1 = (jnp.maximum(z1 + bias_part[:, None, :], 0.0) * live[..., None].astype(f32)).astype(bf16)
-    x1 = lax.all_gather(x1, "row", axis=1, tiled=True)
-    away = sparse_partial(x1[1], w2, to2, row_blocks, True, bf16)
-    back = lax.ppermute(away, "depth", swap)
-    home = sparse_partial(x1[0], w2, to2, row_blocks, True)
-    z2 = (home + back.astype(f32)).astype(bf16)
-    out_share = row_blocks // n_col
-    z2 = lax.all_to_all(z2.reshape(n_col, out_share, rows, block), "col", 0, 0)
-    z2 = z2.astype(f32).sum(0)
-    out = jnp.maximum(z2 + bias2.reshape(out_share, 1, block), 0.0).astype(bf16)
-    return out.transpose(1, 0, 2).reshape(rows, -1)
+    live = jnp.stack([mask2.astype(F32), lax.ppermute(mask2.astype(F32), "depth", swap)])
+    live = lax.dynamic_slice_in_dim(live, first, share, 2)
+    split = (2, n_row // 2, share, rows, block)
+    x1 = first_reduce(
+        [kept0.reshape(split), kept1.reshape(split)],
+        [given0.reshape(split), given1.reshape(split)],
+        bias_part, live,
+    ).reshape(2, col_blocks // 2, rows, block)
+    shape2 = (row_blocks, rows, block)
+    (away,) = sparse_partial(x1[1], w2, to2, core, row_blocks, True, [jax.ShapeDtypeStruct(shape2, BF16)])
+    (home,) = sparse_partial(x1[0], w2, to2, core, row_blocks, True, [jax.ShapeDtypeStruct(shape2, F32)])
+    return second_reduce(home, away, bias2.reshape(row_blocks // n_col, block), n_col)
 
 
 def solution(mesh):
+    near = mesh.shape["depth"] == 2 and mesh.shape["row"] == 4
     return jax.shard_map(
-        exchanged_rows if mesh.shape["depth"] == 2 else gathered_weights,
+        exchanged_rows if near else gathered_weights,
         mesh=mesh,
         in_specs=(
             P("depth", "row"),

time: 269 us -> 160 us (0.59)
  waiting for transfers between devices: 144 us -> 14.5 us
  Pallas kernels: 19.3 us -> 121 us
  blocking collectives: 52.1 us -> 0 us
  between operations: 13.6 us -> 0.28 us
  starting transfers between devices: 11.7 us -> 3.07 us
  other arithmetic: 5.97 us -> 2.36 us
    pallas_call x0 -> x2, Pallas kernels: none -> 101 us  [the longest x1 59.2 us: second_reduce(): pl.pallas_call(functools.partial(second_reduce_kernel, n_col, parts), out...]
    ppermute x3 -> x1, waiting for transfers between devices: 85.2 us -> 14.5 us  [exchanged_rows(): lax.ppermute(mask2.astype(F32), 'depth', swap)]
    all_to_all x1 -> x0, blocking collectives: 52.1 us -> none  [exchanged_rows(): z2 = lax.all_to_all(z2.reshape(n_col, out_share, rows, block), 'col', 0, 0)]
    all_gather x1 -> x0, waiting for transfers between devices: 22.8 us -> none  [exchanged_rows(): x1 = lax.all_gather(x1, 'row', axis=1, tiled=True)]
    all_to_all x1 -> x0, waiting for transfers between devices: 21.6 us -> none  [exchanged_rows(): lax.all_to_all(both.reshape(2, n_row, share, rows, block), 'row', 1, 1)]
    ppermute x1, waiting for transfers between devices: 14.4 us -> 0.01 us  [exchanged_rows(): taken = lax.ppermute(give, 'depth', swap)]
    ppermute x3 -> x1, starting transfers between devices: 4.87 us -> 0.07 us  [exchanged_rows(): lax.ppermute(mask2.astype(F32), 'depth', swap)]
    all_to_all x1 -> x0, starting transfers between devices: 3.74 us -> none  [exchanged_rows(): lax.all_to_all(both.reshape(2, n_row, share, rows, block), 'row', 1, 1)]
  transfers between devices with their start and end apart: 6 -> 2, of which waited for: 6 -> 1; matrix products, arithmetic and copies ran while one was open for 0% -> 0% of each run, Pallas kernels for 4% -> 3%
where the time goes in v2:
time: 160 us
  Pallas kernels  121 us (76%)
  local copies, waits for them, and re-layouts  19 us (12%)
  waiting for transfers between devices  14.5 us (9%)
  starting transfers between devices  3.07 us (2%)
  other arithmetic  2.36 us (1%)
    pallas_call x1, Pallas kernels, second_reduce(): pl.pallas_call(functools.partial(second_reduce_kernel, n_col, parts), out...  59.2 us
    pallas_call x1, Pallas kernels, first_reduce(): pl.pallas_call(functools.partial(first_reduce_kernel, chunks), out_shape=...  42.1 us
    pallas_call x4, Pallas kernels, sparse_partial(): pl.pallas_call(functools.partial(sparse_kernel, per_step, entries, blocke...  19.5 us
    unnamed x30, local copies, waits for them, and re-layouts  15.6 us
    ppermute x1, waiting for transfers between devices, exchanged_rows(): lax.ppermute(mask2.astype(F32), 'depth', swap)  14.5 us
  transfers between devices with their start and end apart: 2, of which 1 were waited for; matrix products, arithmetic and copies ran while one was open for 0% of the time, Pallas kernels for 3%

profile of v2, /device:TPU:0, one launch (start us, length us, event | category | flops | bytes accessed | tf_op | source)
XLA Modules:
  0.0 160.0 jit_solution(4889014887105514898)
XLA Ops:
  0.0 0.9 convert_element_type.8
  0.9 0.1 copy.14
  1.0 1.6 %mul.36 = bf16[128,64,128]{2,1,0:T(8,128)(2,1)S(1)} broadcast(bf16[128,64]{1,0:T(8,128)(2,1)S(1)} %copy.14), dimensions={0,1} | broadcast | bytes 2113536 | tf_op jit(solution)/shard_map/mul | solution.py:353
  2.7 1.3 bitcast_multiply_fusion
  4.0 0.0 copy-start.9
  4.0 0.0 copy-start.10
  4.0 0.0 copy-start.11
  4.0 1.2 constant_dynamic-slice_fusion.1
  5.2 3.0 %collective-permute-start = (bf16[128,4096]{1,0:T(8,128)(2,1)}, bf16[128,4096]{1,0:T(8,128)(2,1)S(1)}, u32[]{:S(2)}, u32[]{:S(2)}) collective-permute-start(bf16[128,4096]{1,0:T(8,128)(2,1)} %get-tuple-element.15), channel_id=1, source_target_pairs={{0,1},{1,0},{2,3},{3,2},{4,5},{5,4},{6,7},{7,6},{8,9},{9,8},{10,11... | collective-permute-start | bytes 3145736 | tf_op jit(solution)/shard_map/ppermute | solution.py:356
  8.2 0.1 copy.15
  8.3 0.1 collective-permute-start.1
  8.4 0.1 dynamic-slice_subtract_fusion
  8.5 0.1 copy.13
  8.5 0.1 reshape.44.cols_ref
  8.7 3.4 %copy-done.1 = bf16[32,8,128,128]{3,2,1,0:T(8,128)(2,1)S(1)} copy-done((bf16[32,8,128,128]{3,2,1,0:T(8,128)(2,1)S(1)}, bf16[32,8,128,128]{3,2,1,0:T(8,128)(2,1)}, u32[]{:S(2)}) %copy-start.1) | copy-done | bytes 8388632
  12.1 4.9 %shard_map.91 = (f32[4,8,128,128]{3,2,1,0:T(8,128)S(1)}, bf16[4,8,128,128]{3,2,1,0:T(8,128)(2,1)S(1)}) custom-call(s32[256]{0:T(256)S(1)} %reshape.44.cols_ref, s32[1]{0:T(128)} %bitcast.core_ref, bf16[128,4096]{1,0:T(8,128)(2,1)S(1)} %get-tuple-element.16.x_ref, bf16[32,8,128,128]{3,2,1,0:T(8,128)(2,1)S(1)} %copy-done.1), custom_call_target="tpu_custom_call" | custom-call | flops 1073741824 | bytes 8388608 | tf_op jit(solution)/shard_map/pallas_call | solution.py:107
  17.0 1.3 copy-done.5
  18.3 0.1 copy.12
  18.4 0.1 reshape.42.cols_ref
  18.5 14.5 %collective-permute-done.1 = f32[128,64]{1,0:T(8,128)S(1)} collective-permute-done((f32[128,64]{1,0:T(8,128)S(1)}, f32[128,64]{1,0:T(8,128)S(1)}, u32[]{:S(2)}, u32[]{:S(2)}) %collective-permute-start.1) | collective-permute-done | bytes 32800 | tf_op jit(solution)/shard_map/ppermute | solution.py:367
  32.9 0.1 dynamic-slice_maximum_fusion.live
  33.1 3.4 %copy-done.2 = bf16[32,8,128,128]{3,2,1,0:T(8,128)(2,1)S(1)} copy-done((bf16[32,8,128,128]{3,2,1,0:T(8,128)(2,1)S(1)}, bf16[32,8,128,128]{3,2,1,0:T(8,128)(2,1)}, u32[]{:S(2)}) %copy-start.2) | copy-done | bytes 8388632
  36.4 4.9 %shard_map.92 = (f32[4,8,128,128]{3,2,1,0:T(8,128)S(1)}, bf16[4,8,128,128]{3,2,1,0:T(8,128)(2,1)S(1)}) custom-call(s32[256]{0:T(256)S(1)} %reshape.44.cols_ref, s32[1]{0:T(128)} %bitcast.core_ref, bf16[128,4096]{1,0:T(8,128)(2,1)S(1)} %collective-permute-done.x_ref, bf16[32,8,128,128]{3,2,1,0:T(8,128)(2,1)S(1)} %copy-done.2), custom_call_target="tpu_custom_call" | custom-call | flops 1073741824 | bytes 8388608 | tf_op jit(solution)/shard_map/pallas_call | solution.py:107
  41.4 1.3 copy-done.6
  42.7 42.1 %first_reduce.1 = bf16[2,2,2,8,128,128]{5,4,3,2,1,0:T(8,128)(2,1)S(1)} custom-call(f32[2,2,8,128,128]{4,3,2,1,0:T(8,128)} %bitcast.20, f32[2,2,8,128,128]{4,3,2,1,0:T(8,128)} %bitcast.21, bf16[2,2,8,128,128]{4,3,2,1,0:T(8,128)(2,1)S(1)} %bitcast.22, bf16[2,2,8,128,128]{4,3,2,1,0:T(8,128)(2,1)S(1)} %bitcast.23, f32[8,128]{1,0:T(8,128)S(1)} %constant_dynamic-slice_fusion.bias, ...), custom_call_target="tpu_custom_call" | custom-call | tf_op jit(solution)/shard_map/first_reduce/pallas_call | solution.py:241
  84.7 0.2 fusion
  85.0 4.8 %shard_map.94.away = bf16[64,128,128]{2,1,0:T(8,128)(2,1)S(1)} custom-call(s32[256]{0:T(256)S(1)} %reshape.42.cols_ref, s32[1]{0:T(128)} %bitcast.core_ref, bf16[32,128,128]{2,1,0:T(8,128)(2,1)S(1)} %bitcast.18, bf16[32,8,128,128]{3,2,1,0:T(8,128)(2,1)S(1)} %bitcast.17), custom_call_target="tpu_custom_call" | custom-call | flops 1073741824 | bytes 8388608 | tf_op jit(solution)/shard_map/pallas_call | solution.py:107
  89.8 3.4 %copy-done.3 = bf16[32,8,128,128]{3,2,1,0:T(8,128)(2,1)S(1)} copy-done((bf16[32,8,128,128]{3,2,1,0:T(8,128)(2,1)S(1)}, bf16[32,8,128,128]{3,2,1,0:T(8,128)(2,1)}, u32[]{:S(2)}) %copy-start.3) | copy-done | bytes 8388632
  93.1 4.8 %shard_map.93.home = f32[64,128,128]{2,1,0:T(8,128)S(1)} custom-call(s32[256]{0:T(256)S(1)} %reshape.42.cols_ref, s32[1]{0:T(128)} %bitcast.core_ref, bf16[32,128,128]{2,1,0:T(8,128)(2,1)S(1)} %bitcast.19, bf16[32,8,128,128]{3,2,1,0:T(8,128)(2,1)S(1)} %copy-done.3), custom_call_target="tpu_custom_call" | custom-call | flops 1073741824 | bytes 8388608 | tf_op jit(solution)/shard_map/pallas_call | solution.py:107
  98.0 1.9 %copy-done.4 = f32[64,128,128]{2,1,0:T(8,128)} copy-done((f32[64,128,128]{2,1,0:T(8,128)}, f32[64,128,128]{2,1,0:T(8,128)S(1)}, u32[]{:S(2)}) %copy-start.4) | copy-done | bytes 4194328
  99.9 59.2 %second_reduce.1 = bf16[128,2048]{1,0:T(8,128)(2,1)S(1)} custom-call(f32[64,128,128]{2,1,0:T(8,128)} %copy-done.4, bf16[64,128,128]{2,1,0:T(8,128)(2,1)S(1)} %shard_map.94.away, f32[16,128]{1,0:T(8,128)S(1)} %bitcast.24), custom_call_target="tpu_custom_call" | custom-call | tf_op jit(solution)/shard_map/second_reduce/pallas_call | solution.py:323
  159.2 0.8 copy.19
  (23 shorter events, 0.1 us)
Async XLA Ops:
  0.0 8.6 %copy-start = (f32[8192]{0:T(1024)S(1)}, f32[8192]{0:T(1024)}, u32[]{:S(2)}) copy-start(f32[8192]{0:T(1024)} %param.13) | copy-start | bytes 98308
  0.0 2.7 %copy-start.8 = (bf16[128,8192]{1,0:T(8,128)(2,1)S(1)}, bf16[128,8192]{1,0:T(8,128)(2,1)}, u32[]{:S(2)}) copy-start(bf16[128,8192]{1,0:T(8,128)(2,1)} %param.9) | copy-start | bytes 6291460
  4.0 4.2 %copy-start.9 = (s32[128,64]{0,1:T(8,128)S(1)}, s32[128,64]{0,1:T(8,128)}, u32[]{:S(2)}) copy-start(s32[128,64]{0,1:T(8,128)} %param.14) | copy-start | bytes 98308
  4.0 4.4 %copy-start.10 = (s32[64,8]{0,1:T(8,128)S(1)}, s32[64,8]{0,1:T(8,128)}, u32[]{:S(2)}) copy-start(s32[64,8]{0,1:T(8,128)} %param.12) | copy-start | bytes 6148
  4.0 4.4 %copy-start.11 = (s32[64,8]{0,1:T(8,128)S(1)}, s32[64,8]{0,1:T(8,128)}, u32[]{:S(2)}) copy-start(s32[64,8]{0,1:T(8,128)} %param.16) | copy-start | bytes 6148
  5.2 27.9 %collective-permute-start = (bf16[128,4096]{1,0:T(8,128)(2,1)}, bf16[128,4096]{1,0:T(8,128)(2,1)S(1)}, u32[]{:S(2)}, u32[]{:S(2)}) collective-permute-start(bf16[128,4096]{1,0:T(8,128)(2,1)} %get-tuple-element.15), channel_id=1, source_target_pairs={{0,1},{1,0},{2,3},{3,2},{4,5},{5,4},{6,7},{7,6},{8,9},{9,8},{10,11... | collective-permute-start | bytes 3145736 | tf_op jit(solution)/shard_map/ppermute | solution.py:356
  8.3 24.7 %collective-permute-start.1 = (f32[128,64]{1,0:T(8,128)S(1)}, f32[128,64]{1,0:T(8,128)S(1)}, u32[]{:S(2)}, u32[]{:S(2)}) collective-permute-start(f32[128,64]{1,0:T(8,128)S(1)} %get-tuple-element.18), channel_id=1, source_target_pairs={{0,1},{1,0},{2,3},{3,2},{4,5},{5,4},{6,7},{7,6},{8,9},{9,8},{10,11... | collective-permute-start | bytes 98312 | tf_op jit(solution)/shard_map/ppermute | solution.py:367
  8.7 3.4 %copy-start.1 = (bf16[32,8,128,128]{3,2,1,0:T(8,128)(2,1)S(1)}, bf16[32,8,128,128]{3,2,1,0:T(8,128)(2,1)}, u32[]{:S(2)}) copy-start(bf16[32,8,128,128]{3,2,1,0:T(8,128)(2,1)} %w_ref.5) | copy-start | bytes 25165828
  17.0 1.3 copy-start.5
  33.0 3.4 %copy-start.2 = (bf16[32,8,128,128]{3,2,1,0:T(8,128)(2,1)S(1)}, bf16[32,8,128,128]{3,2,1,0:T(8,128)(2,1)}, u32[]{:S(2)}) copy-start(bf16[32,8,128,128]{3,2,1,0:T(8,128)(2,1)} %w_ref.5) | copy-start | bytes 25165828
  36.4 48.5 %slice-start = ((s8[8388608]{0:T(1024)(128)(4,1)}), s8[4194304]{0:T(1024)(128)(4,1)S(1)}, s32[]{:S(2)}) async-start(s8[8388608]{0:T(1024)(128)(4,1)} %bitcast.16), calls=%async_computation | async-start | bytes 8388608
  41.4 1.3 copy-start.6
  42.7 42.3 %slice-start.1 = ((s8[8388608]{0:T(1024)(128)(4,1)}), s8[4194304]{0:T(1024)(128)(4,1)S(1)}, s32[]{:S(2)}) async-start(s8[8388608]{0:T(1024)(128)(4,1)} %bitcast.16), calls=%async_computation.1 | async-start | bytes 8388608
  89.8 3.4 %copy-start.3 = (bf16[32,8,128,128]{3,2,1,0:T(8,128)(2,1)S(1)}, bf16[32,8,128,128]{3,2,1,0:T(8,128)(2,1)}, u32[]{:S(2)}) copy-start(bf16[32,8,128,128]{3,2,1,0:T(8,128)(2,1)} %w_ref.7) | copy-start | bytes 25165828
  93.1 6.8 %copy-start.7 = (f32[2048]{0:T(1024)S(1)}, f32[2048]{0:T(1024)}, u32[]{:S(2)}) copy-start(f32[2048]{0:T(1024)} %param.17) | copy-start | bytes 24580
  98.0 1.9 %copy-start.4 = (f32[64,128,128]{2,1,0:T(8,128)}, f32[64,128,128]{2,1,0:T(8,128)S(1)}, u32[]{:S(2)}) copy-start(f32[64,128,128]{2,1,0:T(8,128)S(1)} %shard_map.93.home) | copy-start | bytes 12582916

commit v3 on v2

--- a/solution.py
+++ b/solution.py
@@ -71,7 +71,7 @@
 
     for row in range(per_step):
         if blocked:
-            x = x_ref[row]
+            x = x_ref[:, row].reshape(-1, block)
         else:
             x = x_ref[:, row * block:(row + 1) * block]
         for entry in range(0, entries, 2):
@@ -83,8 +83,10 @@
 
     @pl.when(step == pl.num_programs(0) - 1)
     def _():
-        if len(outs) == 1:
-            outs[0][...] = total[...].astype(outs[0].dtype)
+        if blocked:
+            rows = outs[0].shape[1]
+            for half, out in enumerate(outs):
+                out[...] = total[:, half * rows:(half + 1) * rows].astype(out.dtype)
         else:
             kept, given = outs
             pieces, size = kept.shape[:2]
@@ -97,10 +99,11 @@
 
 def sparse_partial(x, weights, cols, core, out_blocks, blocked, outs):
     stored, entries, block, _ = weights.shape
-    rows = x.shape[1] if blocked else x.shape[0]
+    rows = x.shape[2] if blocked else x.shape[0]
+    lines = 2 * rows if blocked else rows
     per_step = 4 if stored % 4 == 0 else 1
     if blocked:
-        x_spec = pl.BlockSpec((per_step, rows, block), lambda i, *_: (i, 0, 0))
+        x_spec = pl.BlockSpec((2, per_step, rows, block), lambda i, *_: (0, i, 0, 0))
     else:
         x_spec = pl.BlockSpec((rows, per_step * block), lambda i, *_: (0, i))
     zeros = [(lambda n: lambda i, *_: (0,) * n)(len(out.shape)) for out in outs]
@@ -115,13 +118,13 @@
                 pl.BlockSpec((per_step, entries, block, block), lambda i, *_: (i, 0, 0, 0)),
             ],
             out_specs=[pl.BlockSpec(out.shape, zero) for out, zero in zip(outs, zeros)],
-            scratch_shapes=[pltpu.VMEM((out_blocks, rows, block), jnp.float32)],
+            scratch_shapes=[pltpu.VMEM((out_blocks, lines, block), jnp.float32)],
         ),
         compiler_params=pltpu.CompilerParams(
             dimension_semantics=("arbitrary",), vmem_limit_bytes=40 * 1024 * 1024
         ),
         cost_estimate=pl.CostEstimate(
-            flops=2 * rows * weights.size, bytes_accessed=2 * weights.size, transcendentals=0
+            flops=2 * lines * weights.size, bytes_accessed=2 * weights.size, transcendentals=0
         ),
     )(cols.reshape(-1), core.reshape(1), x, weights)
 
@@ -235,7 +238,7 @@
 
 def first_reduce(kept, given, bias, live):
     _, _, share, rows, block = kept[0].shape
-    chunks = 2 if share % 2 == 0 else 1
+    chunks = 4 if share % 4 == 0 else 1
     size = share // chunks
     vmem = pl.BlockSpec(memory_space=pltpu.VMEM)
     return pl.pallas_call(
@@ -264,54 +267,92 @@
     c, d = lax.axis_index("col"), lax.axis_index("depth")
     share, block = out.shape[1] // home.shape[2], home.shape[2]
     size = home.shape[1] // parts
+    last = n_col - 1
+    upper = c // 2
+    inner = c + upper * (last - 2 * c)
     y_peer = {"depth": 1 - d}
-    offsets = sorted(range(1, n_col), key=lambda o: -min(o, n_col - o)) + [0]
-    steps = [(o, p) for o in offsets for p in range(parts)]
-
-    def target(o):
-        return lax.rem(c + o, n_col)
-
-    def y_copy(o, p):
+    steps = [(i, p) for i in range(n_col) for p in range(parts)]
+
+    def mirrored(value):
+        return value + upper * (last - 2 * value)
+
+    def owner(i):
+        end, mid = (3, 2, 1, 0)[i], (2, 0, 3, 1)[i]
+        return mirrored(end + inner * (mid - end))
+
+    def receiver(i):
+        end, mid = (1, 2, 1)[i], (2, 0, 3)[i]
+        return mirrored(end + inner * (mid - end))
+
+    def y_copy(i, p):
         return pltpu.make_async_remote_copy(
-            src_ref=away.at[pl.ds(target(o) * share, share), pl.ds(p * size, size)],
-            dst_ref=y_in.at[o, p],
-            send_sem=send_y.at[o, p], recv_sem=recv_y.at[o, p],
+            src_ref=away.at[pl.ds(owner(i) * share, share), pl.ds(p * size, size)],
+            dst_ref=y_in.at[i, p],
+            send_sem=send_y.at[i, p], recv_sem=recv_y.at[i, p],
             device_id=y_peer, device_id_type=MESH,
         )
 
-    def z_copy(o, p):
+    def z_copy(i, p):
+        slot = 3 * inner if i == 0 else i
         return pltpu.make_async_remote_copy(
-            src_ref=z_out.at[o - 1, p], dst_ref=z_in.at[o - 1, p],
-            send_sem=send_z.at[o - 1, p], recv_sem=recv_z.at[o - 1, p],
-            device_id={"col": target(o)}, device_id_type=MESH,
+            src_ref=z_out.at[i, p], dst_ref=z_in.at[slot, p],
+            send_sem=send_z.at[i, p], recv_sem=recv_z.at[slot, p],
+            device_id={"col": receiver(i)}, device_id_type=MESH,
         )
 
-    greet([y_peer] + [{"col": target(o)} for o in range(1, n_col)])
-    for o, p in steps:
-        y_copy(o, p).start()
-    for o, p in steps:
-        if o == 0:
-            continue
-        y_copy(o, p).wait_recv()
-        z_out[o - 1, p] = (
-            home[pl.ds(target(o) * share, share), p * size:(p + 1) * size]
-            + y_in[o, p].astype(F32)
-        ).astype(BF16)
-        z_copy(o, p).start()
-    for p in range(parts):
-        y_copy(0, p).wait_recv()
-        for o in range(1, n_col):
-            z_copy(o, p).wait_recv()
+    def z_arrival(slot, p):
+        pltpu.make_async_remote_copy(
+            src_ref=z_in.at[slot, p], dst_ref=z_in.at[slot, p],
+            send_sem=send_z.at[0, p], recv_sem=recv_z.at[slot, p],
+            device_id={"col": receiver(0)}, device_id_type=MESH,
+        ).wait_recv()
+
+    greet([y_peer] + [{"col": lax.rem(c + o, n_col)} for o in range(1, n_col)])
+    for i, p in steps:
+        y_copy(i, p).start()
+
+    def near_sum(i, p):
+        return home[pl.ds(owner(i) * share, share), p * size:(p + 1) * size] + y_in[i, p].astype(F32)
+
+    for i, p in steps[:-parts]:
+        y_copy(i, p).wait_recv()
+        if i == 2:
+            @pl.when(inner == 1)
+            def _():
+                z_arrival(0, p)
+                z_out[i, p] = (near_sum(i, p) + z_in[0, p].astype(F32)).astype(BF16)
+
+            @pl.when(inner == 0)
+            def _():
+                z_out[i, p] = near_sum(i, p).astype(BF16)
+        else:
+            z_out[i, p] = near_sum(i, p).astype(BF16)
+        z_copy(i, p).start()
+
+    def finish(p, slots):
+        for slot in slots:
+            z_arrival(slot, p)
         for b in range(share):
-            value = home[c * share + b, p * size:(p + 1) * size] + y_in[0, p, b].astype(F32)
-            for o in range(1, n_col):
-                value += z_in[o - 1, p, b].astype(F32)
+            value = home[c * share + b, p * size:(p + 1) * size] + y_in[n_col - 1, p, b].astype(F32)
+            for slot in slots:
+                value += z_in[slot, p, b].astype(F32)
             value = jnp.maximum(value + bias[b:b + 1, :], 0.0)
             out[p * size:(p + 1) * size, b * block:(b + 1) * block] = value.astype(BF16)
-    for o, p in steps:
-        y_copy(o, p).wait_send()
-        if o:
-            z_copy(o, p).wait_send()
+
+    for p in range(parts):
+        y_copy(n_col - 1, p).wait_recv()
+
+        @pl.when(inner == 1)
+        def _():
+            finish(p, (1, 2, 3))
+
+        @pl.when(inner == 0)
+        def _():
+            finish(p, (1, 2))
+    for i, p in steps:
+        y_copy(i, p).wait_send()
+        if i < n_col - 1:
+            z_copy(i, p).wait_send()
 
 
 def second_reduce(home, away, bias, n_col):
@@ -328,11 +369,11 @@
         scratch_shapes=[
             pltpu.VMEM((n_col, parts, share, size, block), BF16),
             pltpu.VMEM((n_col - 1, parts, share, size, block), BF16),
-            pltpu.VMEM((n_col - 1, parts, share, size, block), BF16),
+            pltpu.VMEM((n_col, parts, share, size, block), BF16),
             pltpu.SemaphoreType.DMA((n_col, parts)),
             pltpu.SemaphoreType.DMA((n_col, parts)),
             pltpu.SemaphoreType.DMA((n_col - 1, parts)),
-            pltpu.SemaphoreType.DMA((n_col - 1, parts)),
+            pltpu.SemaphoreType.DMA((n_col, parts)),
         ],
         compiler_params=pltpu.CompilerParams(
             collective_id=2, has_side_effects=True, vmem_limit_bytes=48 * 1024 * 1024
@@ -373,13 +414,13 @@
         bias_part, live,
     ).reshape(2, col_blocks // 2, rows, block)
     shape2 = (row_blocks, rows, block)
-    (away,) = sparse_partial(x1[1], w2, to2, core, row_blocks, True, [jax.ShapeDtypeStruct(shape2, BF16)])
-    (home,) = sparse_partial(x1[0], w2, to2, core, row_blocks, True, [jax.ShapeDtypeStruct(shape2, F32)])
+    outs2 = [jax.ShapeDtypeStruct(shape2, F32), jax.ShapeDtypeStruct(shape2, BF16)]
+    home, away = sparse_partial(x1, w2, to2, core, row_blocks, True, outs2)
     return second_reduce(home, away, bias2.reshape(row_blocks // n_col, block), n_col)
 
 
 def solution(mesh):
-    near = mesh.shape["depth"] == 2 and mesh.shape["row"] == 4
+    near = mesh.shape["depth"] == 2 and mesh.shape["row"] == 4 and mesh.shape["col"] == 4
     return jax.shard_map(
         exchanged_rows if near else gathered_weights,
         mesh=mesh,

time: 160 us -> 149 us (0.931)
  Pallas kernels: 121 us -> 113 us
  local copies, waits for them, and re-layouts: 19 us -> 15.5 us
    pallas_call x1, Pallas kernels: 59.2 us -> 51.9 us  [second_reduce(): pl.pallas_call(functools.partial(second_reduce_kernel, n_col, parts), out...]
    unnamed x30 -> x24, local copies, waits for them, and re-layouts: 15.6 us -> 12.3 us
    pallas_call x1, Pallas kernels: 42.1 us -> 40.4 us  [first_reduce(): pl.pallas_call(functools.partial(first_reduce_kernel, chunks), out_shape=...]
    pallas_call x4 -> x3, Pallas kernels: 19.5 us -> 20.6 us  [sparse_partial(): pl.pallas_call(functools.partial(sparse_kernel, per_step, entries, blocke...]
where the time goes in v3:
time: 149 us; the launch traced here: 148 us
  Pallas kernels  113 us (76%)
  local copies, waits for them, and re-layouts  15.5 us (10%)
  waiting for transfers between devices  14.5 us (10%)
  starting transfers between devices  3.07 us (2%)
  other arithmetic  2.36 us (2%)
    pallas_call x1, Pallas kernels, second_reduce(): pl.pallas_call(functools.partial(second_reduce_kernel, n_col, parts), out...  51.9 us
    pallas_call x1, Pallas kernels, first_reduce(): pl.pallas_call(functools.partial(first_reduce_kernel, chunks), out_shape=...  40.4 us
    pallas_call x3, Pallas kernels, sparse_partial(): pl.pallas_call(functools.partial(sparse_kernel, per_step, entries, blocke...  20.6 us
    ppermute x1, waiting for transfers between devices, exchanged_rows(): lax.ppermute(mask2.astype(F32), 'depth', swap)  14.4 us
    unnamed x24, local copies, waits for them, and re-layouts  12.3 us
    ppermute x1, starting transfers between devices, exchanged_rows(): taken = lax.ppermute(give, 'depth', swap)  3 us
  transfers between devices with their start and end apart: 2, of which 1 were waited for; matrix products, arithmetic and copies ran while one was open for 0% of the time, Pallas kernels for 3%

profile of v3, /device:TPU:0, one launch (start us, length us, event | category | flops | bytes accessed | tf_op | source)
XLA Modules:
  0.0 148.4 jit_solution(8769401115387340412)
XLA Ops:
  0.0 0.9 convert_element_type.8
  0.9 0.1 copy.14
  1.0 1.6 %mul.36 = bf16[128,64,128]{2,1,0:T(8,128)(2,1)S(1)} broadcast(bf16[128,64]{1,0:T(8,128)(2,1)S(1)} %copy.14), dimensions={0,1} | broadcast | bytes 2113536 | tf_op jit(solution)/shard_map/mul | solution.py:394
  2.7 1.3 bitcast_multiply_fusion
  4.0 0.0 copy-start.8
  4.0 0.0 copy-start.9
  4.0 0.0 copy-start.10
  4.0 1.2 constant_dynamic-slice_fusion.1
  5.2 3.0 %collective-permute-start = (bf16[128,4096]{1,0:T(8,128)(2,1)}, bf16[128,4096]{1,0:T(8,128)(2,1)S(1)}, u32[]{:S(2)}, u32[]{:S(2)}) collective-permute-start(bf16[128,4096]{1,0:T(8,128)(2,1)} %get-tuple-element.17), channel_id=1, source_target_pairs={{0,1},{1,0},{2,3},{3,2},{4,5},{5,4},{6,7},{7,6},{8,9},{9,8},{10,11... | collective-permute-start | bytes 3145736 | tf_op jit(solution)/shard_map/ppermute | solution.py:397
  8.2 0.1 copy.15
  8.3 0.1 collective-permute-start.1
  8.4 0.1 dynamic-slice_subtract_fusion
  8.5 0.1 copy.13
  8.5 0.1 reshape.40.cols_ref
  8.7 0.0 copy-start.1
  8.7 3.4 %copy-done.1 = bf16[32,8,128,128]{3,2,1,0:T(8,128)(2,1)S(1)} copy-done((bf16[32,8,128,128]{3,2,1,0:T(8,128)(2,1)S(1)}, bf16[32,8,128,128]{3,2,1,0:T(8,128)(2,1)}, u32[]{:S(2)}) %copy-start.1) | copy-done | bytes 8388632
  12.0 4.9 %shard_map.91 = (f32[4,8,128,128]{3,2,1,0:T(8,128)S(1)}, bf16[4,8,128,128]{3,2,1,0:T(8,128)(2,1)S(1)}) custom-call(s32[256]{0:T(256)S(1)} %reshape.40.cols_ref, s32[1]{0:T(128)} %bitcast.core_ref, bf16[128,4096]{1,0:T(8,128)(2,1)S(1)} %get-tuple-element.18.x_ref, bf16[32,8,128,128]{3,2,1,0:T(8,128)(2,1)S(1)} %copy-done.1), custom_call_target="tpu_custom_call" | custom-call | flops 1073741824 | bytes 8388608 | tf_op jit(solution)/shard_map/pallas_call | solution.py:110
  17.0 1.3 copy-done.4
  18.3 0.1 copy.12
  18.4 0.1 reshape.38.cols_ref
  18.5 14.4 %collective-permute-done.1 = f32[128,64]{1,0:T(8,128)S(1)} collective-permute-done((f32[128,64]{1,0:T(8,128)S(1)}, f32[128,64]{1,0:T(8,128)S(1)}, u32[]{:S(2)}, u32[]{:S(2)}) %collective-permute-start.1) | collective-permute-done | bytes 32800 | tf_op jit(solution)/shard_map/ppermute | solution.py:408
  32.9 0.1 dynamic-slice_maximum_fusion.live
  33.0 0.0 copy-start.2
  33.0 3.4 %copy-done.2 = bf16[32,8,128,128]{3,2,1,0:T(8,128)(2,1)S(1)} copy-done((bf16[32,8,128,128]{3,2,1,0:T(8,128)(2,1)S(1)}, bf16[32,8,128,128]{3,2,1,0:T(8,128)(2,1)}, u32[]{:S(2)}) %copy-start.2) | copy-done | bytes 8388632
  36.4 4.9 %shard_map.92 = (f32[4,8,128,128]{3,2,1,0:T(8,128)S(1)}, bf16[4,8,128,128]{3,2,1,0:T(8,128)(2,1)S(1)}) custom-call(s32[256]{0:T(256)S(1)} %reshape.40.cols_ref, s32[1]{0:T(128)} %bitcast.core_ref, bf16[128,4096]{1,0:T(8,128)(2,1)S(1)} %collective-permute-done.x_ref, bf16[32,8,128,128]{3,2,1,0:T(8,128)(2,1)S(1)} %copy-done.2), custom_call_target="tpu_custom_call" | custom-call | flops 1073741824 | bytes 8388608 | tf_op jit(solution)/shard_map/pallas_call | solution.py:110
  41.3 1.3 copy-done.5
  42.7 40.4 %first_reduce.1 = bf16[2,2,2,8,128,128]{5,4,3,2,1,0:T(8,128)(2,1)S(1)} custom-call(f32[2,2,8,128,128]{4,3,2,1,0:T(8,128)} %bitcast.16, f32[2,2,8,128,128]{4,3,2,1,0:T(8,128)} %bitcast.17, bf16[2,2,8,128,128]{4,3,2,1,0:T(8,128)(2,1)S(1)} %bitcast.18, bf16[2,2,8,128,128]{4,3,2,1,0:T(8,128)(2,1)S(1)} %bitcast.19, f32[8,128]{1,0:T(8,128)S(1)} %constant_dynamic-slice_fusion.bias, ...), custom_call_target="tpu_custom_call" | custom-call | tf_op jit(solution)/shard_map/first_reduce/pallas_call | solution.py:244
  83.1 0.0 copy-start.6
  83.1 10.7 %shard_map.93 = (f32[64,128,128]{2,1,0:T(8,128)S(1)}, bf16[64,128,128]{2,1,0:T(8,128)(2,1)S(1)}) custom-call(s32[256]{0:T(256)S(1)} %reshape.38.cols_ref, s32[1]{0:T(128)} %bitcast.core_ref, bf16[2,32,128,128]{3,2,1,0:T(8,128)(2,1)S(1)} %bitcast.15, bf16[32,8,128,128]{3,2,1,0:T(8,128)(2,1)} %w_ref.5), custom_call_target="tpu_custom_call" | custom-call | flops 2147483648 | bytes 8388608 | tf_op jit(solution)/shard_map/pallas_call | solution.py:110
  93.8 1.9 %copy-done.3 = f32[64,128,128]{2,1,0:T(8,128)} copy-done((f32[64,128,128]{2,1,0:T(8,128)}, f32[64,128,128]{2,1,0:T(8,128)S(1)}, u32[]{:S(2)}) %copy-start.3) | copy-done | bytes 4194328
  95.8 51.9 %second_reduce.1 = bf16[128,2048]{1,0:T(8,128)(2,1)S(1)} custom-call(f32[64,128,128]{2,1,0:T(8,128)} %copy-done.3, bf16[64,128,128]{2,1,0:T(8,128)(2,1)S(1)} %get-tuple-element.16.away, f32[16,128]{1,0:T(8,128)S(1)} %bitcast.20), custom_call_target="tpu_custom_call" | custom-call | tf_op jit(solution)/shard_map/second_reduce/pallas_call | solution.py:364
  147.6 0.8 copy.19
  (14 shorter events, 0.0 us)
Async XLA Ops:
  0.0 8.6 %copy-start = (f32[8192]{0:T(1024)S(1)}, f32[8192]{0:T(1024)}, u32[]{:S(2)}) copy-start(f32[8192]{0:T(1024)} %param.13) | copy-start | bytes 98308
  0.0 2.7 %copy-start.7 = (bf16[128,8192]{1,0:T(8,128)(2,1)S(1)}, bf16[128,8192]{1,0:T(8,128)(2,1)}, u32[]{:S(2)}) copy-start(bf16[128,8192]{1,0:T(8,128)(2,1)} %param.9) | copy-start | bytes 6291460
  4.0 4.2 %copy-start.8 = (s32[128,64]{0,1:T(8,128)S(1)}, s32[128,64]{0,1:T(8,128)}, u32[]{:S(2)}) copy-start(s32[128,64]{0,1:T(8,128)} %param.14) | copy-start | bytes 98308
  4.0 4.4 %copy-start.9 = (s32[64,8]{0,1:T(8,128)S(1)}, s32[64,8]{0,1:T(8,128)}, u32[]{:S(2)}) copy-start(s32[64,8]{0,1:T(8,128)} %param.12) | copy-start | bytes 6148
  4.0 4.4 %copy-start.10 = (s32[64,8]{0,1:T(8,128)S(1)}, s32[64,8]{0,1:T(8,128)}, u32[]{:S(2)}) copy-start(s32[64,8]{0,1:T(8,128)} %param.16) | copy-start | bytes 6148
  5.2 27.9 %collective-permute-start = (bf16[128,4096]{1,0:T(8,128)(2,1)}, bf16[128,4096]{1,0:T(8,128)(2,1)S(1)}, u32[]{:S(2)}, u32[]{:S(2)}) collective-permute-start(bf16[128,4096]{1,0:T(8,128)(2,1)} %get-tuple-element.17), channel_id=1, source_target_pairs={{0,1},{1,0},{2,3},{3,2},{4,5},{5,4},{6,7},{7,6},{8,9},{9,8},{10,11... | collective-permute-start | bytes 3145736 | tf_op jit(solution)/shard_map/ppermute | solution.py:397
  8.3 24.7 %collective-permute-start.1 = (f32[128,64]{1,0:T(8,128)S(1)}, f32[128,64]{1,0:T(8,128)S(1)}, u32[]{:S(2)}, u32[]{:S(2)}) collective-permute-start(f32[128,64]{1,0:T(8,128)S(1)} %get-tuple-element.20), channel_id=1, source_target_pairs={{0,1},{1,0},{2,3},{3,2},{4,5},{5,4},{6,7},{7,6},{8,9},{9,8},{10,11... | collective-permute-start | bytes 98312 | tf_op jit(solution)/shard_map/ppermute | solution.py:408
  8.7 3.4 %copy-start.1 = (bf16[32,8,128,128]{3,2,1,0:T(8,128)(2,1)S(1)}, bf16[32,8,128,128]{3,2,1,0:T(8,128)(2,1)}, u32[]{:S(2)}) copy-start(bf16[32,8,128,128]{3,2,1,0:T(8,128)(2,1)} %w_ref.4) | copy-start | bytes 25165828
  17.0 1.3 copy-start.4
  33.0 3.4 %copy-start.2 = (bf16[32,8,128,128]{3,2,1,0:T(8,128)(2,1)S(1)}, bf16[32,8,128,128]{3,2,1,0:T(8,128)(2,1)}, u32[]{:S(2)}) copy-start(bf16[32,8,128,128]{3,2,1,0:T(8,128)(2,1)} %w_ref.4) | copy-start | bytes 25165828
  41.3 1.3 copy-start.5
  83.1 12.7 %copy-start.6 = (f32[2048]{0:T(1024)S(1)}, f32[2048]{0:T(1024)}, u32[]{:S(2)}) copy-start(f32[2048]{0:T(1024)} %param.17) | copy-start | bytes 24580
  93.8 2.0 %copy-start.3 = (f32[64,128,128]{2,1,0:T(8,128)}, f32[64,128,128]{2,1,0:T(8,128)S(1)}, u32[]{:S(2)}) copy-start(f32[64,128,128]{2,1,0:T(8,128)S(1)} %get-tuple-element.15.home) | copy-start | bytes 12582916
